TPU v7x, 32 devices: a whole 2x2x4 slice. The times are simulated.
32 devices in a mesh: gx: 4 (over y, x), gy: 4 (over z), gz: 2 (over core).
Axes of the slice: x: 2, y: 2, z: 4, core: 2. Of those that a mesh axis runs over, the one named last changes fastest.
Arguments:
- labels: int32 [16, 32], P('gx', 'gy'), may hold values from 0 to 2
- phase_noise: float32 [4, 16, 32, 256], P(None, 'gx', 'gy', 'gz'), may hold values from 0.05 to 0.6
- potentials: float32 [2, 16, 32, 256], P(None, 'gx', 'gy', 'gz'), may hold values from -3 to 3
- frame_shift: int32 [2], replicated, may hold values from 1 to 8, as said below
Outputs:
- final_phases: float32 [4, 16, 32, 256], P(None, 'gx', 'gy', 'gz')
- final_potentials: float32 [2, 16, 32, 256], P(None, 'gx', 'gy', 'gz')
Inputs may be any that keep to these rules, and one draw needn't show every extreme that they name: `frame_shift`: each entry lies from 1 to 8, and at least one entry equals 8.
All inputs are finite; a program needn't handle non-finite values.
Results may differ from a plain program's by a relative error of at most 0.0001.
Values sent between devices are 32-bit elements; how exact they have to be, the bound alone decides.
A program may use at most 64 MiB of HBM per device.

v0:
```python
import math

import jax
import jax.numpy as jnp
from jax import lax
from jax.sharding import PartitionSpec as P

SHIFT_MAX = 8


interface_width = 4.0
relax_time = 1.0
time_step = 0.12
obstacle_coef = 16.0 / (math.pi * math.pi)
normal_floor = 0.25
surface_table = [
    [0.0, 1.0, 1.2, 0.9],
    [1.0, 0.0, 1.1, 1.0],
    [1.2, 1.1, 0.0, 0.8],
    [0.9, 1.0, 0.8, 0.0],
]
compositions = [[0.8, 0.1], [0.1, 0.8], [0.1, 0.1], [0.33, 0.33]]
latent_heat = [1.0, 0.9, 1.1, 0.0]
mobility_solid = 0.1
mobility_liquid = 1.0
trapping_coef = math.pi * 4.0 / 4.0
undercool_span = 2.0


def shifted(value, axis, steps):
    count = lax.axis_size(axis)
    leading, last = (max(0, -steps), min(count, count - steps))
    return lax.ppermute(value, axis, [(source, source + steps) for source in range(leading, last)])


def with_halo(block, sides, width):
    for axis, dim in sides:
        count = lax.axis_size(axis)
        forward = [(i, i + 1) for i in range(count - 1)]
        forward.append((count - 1, 0))
        backward = [(target, source) for source, target in forward]
        low = lax.ppermute(
            lax.slice_in_dim(block, block.shape[dim] - width, None, axis=dim), axis, forward
        )
        high = lax.ppermute(lax.slice_in_dim(block, 0, width, axis=dim), axis, backward)
        block = jnp.concatenate([low, block, high], axis=dim)
    return block


def laplacian(padded):
    center = padded[:, 1:-1, 1:-1, 1:-1]
    total = padded[:, 2:, 1:-1, 1:-1] + padded[:, :-2, 1:-1, 1:-1]
    total = total + padded[:, 1:-1, 2:, 1:-1] + padded[:, 1:-1, :-2, 1:-1]
    total = total + padded[:, 1:-1, 1:-1, 2:] + padded[:, 1:-1, 1:-1, :-2]
    return total - 6.0 * center


def gradient(padded):
    along_x = 0.5 * (padded[:, 2:, 1:-1, 1:-1] - padded[:, :-2, 1:-1, 1:-1])
    along_y = 0.5 * (padded[:, 1:-1, 2:, 1:-1] - padded[:, 1:-1, :-2, 1:-1])
    along_z = 0.5 * (padded[:, 1:-1, 1:-1, 2:] - padded[:, 1:-1, 1:-1, :-2])
    return (along_x, along_y, along_z)


def phase_part(padded_phase, chem_pot, undercool):
    interior = padded_phase[:, 1:-1, 1:-1, 1:-1]
    curve = laplacian(padded_phase)
    drive_list = []
    for a in range(4):
        bend = jnp.zeros_like(interior[0])
        contact = jnp.zeros_like(interior[0])
        for b in range(4):
            if b != a:
                bend = bend + surface_table[a][b] * (
                    interior[b] * curve[a] - interior[a] * curve[b]
                )
                contact = contact + surface_table[a][b] * interior[b]
        variation = -interface_width * bend + obstacle_coef / interface_width * contact
        variation = variation - (
            compositions[a][0] * chem_pot[0] + compositions[a][1] * chem_pot[1]
        )
        variation = variation + latent_heat[a] * undercool
        drive_list.append(variation)
    variation = jnp.stack(drive_list)
    average = jnp.mean(variation, axis=0)
    growth_rate = -(variation - average) / (relax_time * interface_width)
    clipped = jnp.clip(interior + time_step * growth_rate, 0.0, 1.0)
    updated = clipped / jnp.sum(clipped, axis=0)
    change = (updated - interior) / time_step
    slopes = gradient(padded_phase)
    magnitude = jnp.sqrt(slopes[0] * slopes[0] + slopes[1] * slopes[1] + slopes[2] * slopes[2])
    inverse_norm = 1.0 / jnp.maximum(magnitude, normal_floor)
    carried = [4.0 * interior[a] * interior[3] * change[a] * inverse_norm[a] for a in range(3)]
    currents = []
    for k in range(2):
        for d in range(3):
            total = jnp.zeros_like(interior[0])
            for a in range(3):
                total = (
                    total + (compositions[3][k] - compositions[a][k]) * carried[a] * slopes[d][a]
                )
            currents.append(-trapping_coef * total)
    return (updated, change, jnp.stack(currents))


def neighbor(block, d, offset):
    pieces = [slice(1, -1), slice(1, -1), slice(1, -1)]
    pieces[d] = slice(1 + offset, block.shape[d] - 1 + offset)
    return block[tuple(pieces)]


def potential_part(padded_pot, padded_mob, padded_flux, change):
    center_mob = padded_mob[1:-1, 1:-1, 1:-1]
    results = []
    for k in range(2):
        chem = padded_pot[k]
        center = chem[1:-1, 1:-1, 1:-1]
        divergence = jnp.zeros_like(center)
        for d in range(3):
            current = padded_flux[3 * k + d]
            upper_face = (
                0.5 * (neighbor(padded_mob, d, 1) + center_mob) * (neighbor(chem, d, 1) - center)
            )
            upper_face = upper_face - 0.5 * (neighbor(current, d, 1) + neighbor(current, d, 0))
            lower_face = (
                0.5 * (center_mob + neighbor(padded_mob, d, -1)) * (center - neighbor(chem, d, -1))
            )
            lower_face = lower_face - 0.5 * (neighbor(current, d, 0) + neighbor(current, d, -1))
            divergence = divergence + (upper_face - lower_face)
        source = jnp.zeros_like(center)
        for a in range(4):
            source = source + compositions[a][k] * change[a]
        results.append(center + time_step * (divergence - source))
    return jnp.stack(results)


def clamp_ends(block, margin, lower, upper):
    inner_part = block[..., margin:-margin]
    first_plane = block[..., margin : margin + 1]
    last_plane = block[..., -margin - 1 : -margin]
    low_side = jnp.where(
        lower, jnp.broadcast_to(first_plane, block[..., :margin].shape), block[..., :margin]
    )
    high_side = jnp.where(
        upper, jnp.broadcast_to(last_plane, block[..., -margin:].shape), block[..., -margin:]
    )
    return jnp.concatenate([low_side, inner_part, high_side], axis=-1)


def move_frame(fields, offset, upper):
    tail = shifted(fields[..., :SHIFT_MAX], "gz", -1)
    rows_x = fields.shape[1]
    rows_y = fields.shape[2]
    far = jnp.concatenate(
        [
            jnp.zeros((3, rows_x, rows_y, SHIFT_MAX), jnp.float32),
            jnp.ones((1, rows_x, rows_y, SHIFT_MAX), jnp.float32),
            jnp.zeros((2, rows_x, rows_y, SHIFT_MAX), jnp.float32),
        ],
        axis=0,
    )
    tail = jnp.where(upper, far, tail)
    joined = jnp.concatenate([fields, tail], axis=3)
    return lax.dynamic_slice_in_dim(joined, offset, fields.shape[3], axis=3)


def advance(window, margin, position, planes, total_planes, front, lower, upper):
    inner = window[:, 1:-1, 1:-1, 1:-1]
    reach = margin - 1
    wider_index = position * planes + jnp.arange(-reach, planes + reach, dtype=jnp.int32)
    undercool_wide = undercool_span * (wider_index.astype(jnp.float32) + 0.5 - front) / total_planes
    updated, change, currents = phase_part(window[:4], inner[4:], undercool_wide)
    currents = clamp_ends(currents, reach, lower, upper)
    mobility = mobility_solid + (mobility_liquid - mobility_solid) * inner[3]
    chem_new = potential_part(inner[4:], mobility, currents, change[:, 1:-1, 1:-1, 1:-1])
    return jnp.concatenate([updated[:, 1:-1, 1:-1, 1:-1], chem_new], axis=0)


def on_device(labels, phase_noise, potentials, frame_shift):
    planes = phase_noise.shape[3]
    layers = lax.axis_size("gz")
    total_planes = planes * layers
    front = total_planes // 2
    position = lax.axis_index("gz")
    lower = position == 0
    upper = position == layers - 1
    zindex = position * planes + jnp.arange(planes, dtype=jnp.int32)
    solid = zindex < front
    onehot = []
    for a in range(3):
        onehot.append(((labels == a)[:, :, None] & solid[None, None, :]).astype(jnp.float32))
    onehot.append(
        jnp.broadcast_to((~solid)[None, None, :], phase_noise.shape[1:]).astype(jnp.float32)
    )
    initial = jnp.stack(onehot) + phase_noise
    phases = initial / jnp.sum(initial, axis=0)
    fields = jnp.concatenate([phases, potentials], axis=0)

    def narrow_step(current_fields):
        rim = with_halo(current_fields, (("gx", 1), ("gy", 2), ("gz", 3)), 2)
        rim = clamp_ends(rim, 2, lower, upper)
        return advance(rim, 2, position, planes, total_planes, front, lower, upper)

    fields = narrow_step(fields)
    fields = move_frame(fields, frame_shift[0], upper)
    wide = with_halo(fields, (("gx", 1), ("gy", 2), ("gz", 3)), 4)
    wide = clamp_ends(wide, 4, lower, upper)
    middle = advance(wide, 4, position, planes, total_planes, front, lower, upper)
    middle = clamp_ends(middle, 2, lower, upper)
    fields = advance(middle, 2, position, planes, total_planes, front, lower, upper)
    fields = move_frame(fields, frame_shift[1], upper)
    fields = narrow_step(fields)
    return (fields[:4], fields[4:])


def solution(mesh):
    placed = (P("gx", "gy"), P(None, "gx", "gy", "gz"), P(None, "gx", "gy", "gz"), P())
    return jax.shard_map(
        on_device,
        mesh=mesh,
        in_specs=placed,
        out_specs=(P(None, "gx", "gy", "gz"), P(None, "gx", "gy", "gz")),
        check_vma=False,
    )
```

profile of v0, /device:TPU:0, one launch (start us, length us, event | category | flops | bytes accessed | tf_op | source)
XLA Modules:
  0.0 99.1 jit_solution(8197517964295308717)
XLA Ops:
  0.6 0.7 broadcast_compare_fusion.2
  1.4 0.9 fusion.267
  2.3 0.9 broadcast_divide_fusion.4
  3.2 0.8 fusion.86
  3.9 3.0 %collective-permute-start = (f32[6,2,8,128]{3,2,1,0:T(8,128)S(1)}, f32[6,2,8,128]{3,2,1,0:T(8,128)S(1)}, u32[]{:S(2)}, u32[]{:S(2)}) collective-permute-start(f32[6,2,8,128]{3,2,1,0:T(8,128)S(1)} %get-tuple-element.169), channel_id=1, source_target_pairs={{0,8},{8,16},{16,24},{24,0},{1,9},{9,17},{17,25},{25,1},{2,10},{10... | collective-permute-start | bytes 147464 | tf_op jit(solution)/shard_map/ppermute | solution.py:42
  6.9 1.0 %collective-permute-start.1 = (f32[6,2,8,128]{3,2,1,0:T(8,128)S(1)}, f32[6,2,8,128]{3,2,1,0:T(8,128)S(1)}, u32[]{:S(2)}, u32[]{:S(2)}) collective-permute-start(f32[6,2,8,128]{3,2,1,0:T(8,128)S(1)} %get-tuple-element.170), channel_id=1, source_target_pairs={{8,0},{16,8},{24,16},{0,24},{9,1},{17,9},{25,17},{1,25},{10,2},{18... | collective-permute-start | bytes 147464 | tf_op jit(solution)/shard_map/ppermute | solution.py:45
  7.9 2.0 %collective-permute-done = f32[6,2,8,128]{3,2,1,0:T(8,128)S(1)} collective-permute-done((f32[6,2,8,128]{3,2,1,0:T(8,128)S(1)}, f32[6,2,8,128]{3,2,1,0:T(8,128)S(1)}, u32[]{:S(2)}, u32[]{:S(2)}) %collective-permute-start) | collective-permute-done | bytes 49184 | tf_op jit(solution)/shard_map/ppermute | solution.py:42
  9.9 1.1 %collective-permute-done.1 = f32[6,2,8,128]{3,2,1,0:T(8,128)S(1)} collective-permute-done((f32[6,2,8,128]{3,2,1,0:T(8,128)S(1)}, f32[6,2,8,128]{3,2,1,0:T(8,128)S(1)}, u32[]{:S(2)}, u32[]{:S(2)}) %collective-permute-start.1) | collective-permute-done | bytes 49184 | tf_op jit(solution)/shard_map/ppermute | solution.py:45
  11.0 0.8 pad_maximum_fusion.17
  11.8 1.6 %collective-permute-start.2 = (f32[6,8,2,128]{3,1,2,0:T(8,128)S(1)}, f32[6,8,2,128]{3,1,2,0:T(8,128)S(1)}, u32[]{:S(2)}, u32[]{:S(2)}) collective-permute-start(f32[6,8,2,128]{3,1,2,0:T(8,128)S(1)} %copy.424), channel_id=1, source_target_pairs={{0,2},{2,4},{4,6},{6,0},{1,3},{3,5},{5,7},{7,1},{8,10},{10,12},{12... | collective-permute-start | bytes 147464 | tf_op jit(solution)/shard_map/ppermute | solution.py:42
  13.5 2.3 %collective-permute-start.3 = (f32[6,8,2,128]{3,1,2,0:T(8,128)S(1)}, f32[6,8,2,128]{3,1,2,0:T(8,128)S(1)}, u32[]{:S(2)}, u32[]{:S(2)}) collective-permute-start(f32[6,8,2,128]{3,1,2,0:T(8,128)S(1)} %copy.425), channel_id=1, source_target_pairs={{2,0},{4,2},{6,4},{0,6},{3,1},{5,3},{7,5},{1,7},{10,8},{12,10},{14... | collective-permute-start | bytes 147464 | tf_op jit(solution)/shard_map/ppermute | solution.py:45
  15.8 2.1 %collective-permute-done.2 = f32[6,8,2,128]{3,1,2,0:T(8,128)S(1)} collective-permute-done((f32[6,8,2,128]{3,1,2,0:T(8,128)S(1)}, f32[6,8,2,128]{3,1,2,0:T(8,128)S(1)}, u32[]{:S(2)}, u32[]{:S(2)}) %collective-permute-start.2) | collective-permute-done | bytes 49184 | tf_op jit(solution)/shard_map/ppermute | solution.py:42
  19.7 0.6 copy.403
  24.1 1.3 %collective-permute-start.6 = (f32[6,4,8,8]{3,2,1,0:T(8,128)S(1)}, f32[6,4,8,8]{3,2,1,0:T(8,128)S(1)}, u32[]{:S(2)}, u32[]{:S(2)}) collective-permute-start(f32[6,4,8,8]{3,2,1,0:T(8,128)S(1)} %bitcast.148), channel_id=1, source_target_pairs={{1,0},{3,2},{5,4},{7,6},{9,8},{11,10},{13,12},{15,14},{17,16},{19,... | collective-permute-start | bytes 18440 | tf_op jit(solution)/shard_map/ppermute | solution.py:33
  25.4 0.6 fusion.292
  28.1 2.4 %collective-permute-start.8 = (f32[6,4,8,128]{3,2,1,0:T(8,128)S(1)}, f32[6,4,8,128]{3,2,1,0:T(8,128)S(1)}, u32[]{:S(2)}, u32[]{:S(2)}) collective-permute-start(f32[6,4,8,128]{3,2,1,0:T(8,128)S(1)} %fusion.19), channel_id=1, source_target_pairs={{8,0},{16,8},{24,16},{0,24},{9,1},{17,9},{25,17},{1,25},{10,2},{18... | collective-permute-start | bytes 294920 | tf_op jit(solution)/shard_map/ppermute | solution.py:45
  30.7 3.1 %collective-permute-done.8 = f32[6,4,8,128]{3,2,1,0:T(8,128)S(1)} collective-permute-done((f32[6,4,8,128]{3,2,1,0:T(8,128)S(1)}, f32[6,4,8,128]{3,2,1,0:T(8,128)S(1)}, u32[]{:S(2)}, u32[]{:S(2)}) %collective-permute-start.8) | collective-permute-done | bytes 98336 | tf_op jit(solution)/shard_map/ppermute | solution.py:45
  33.8 3.2 %collective-permute-done.7 = f32[6,4,8,128]{3,2,1,0:T(8,128)S(1)} collective-permute-done((f32[6,4,8,128]{3,2,1,0:T(8,128)S(1)}, f32[6,4,8,128]{3,2,1,0:T(8,128)S(1)}, u32[]{:S(2)}, u32[]{:S(2)}) %collective-permute-start.7) | collective-permute-done | bytes 98336 | tf_op jit(solution)/shard_map/ppermute | solution.py:42
  37.0 1.1 %collective-permute-start.9 = (f32[6,12,4,128]{3,2,1,0:T(4,128)S(1)}, f32[6,12,4,128]{3,2,1,0:T(4,128)S(1)}, u32[]{:S(2)}, u32[]{:S(2)}) collective-permute-start(f32[6,12,4,128]{3,2,1,0:T(4,128)S(1)} %get-tuple-element.157), channel_id=1, source_target_pairs={{0,2},{2,4},{4,6},{6,0},{1,3},{3,5},{5,7},{7,1},{8,10},{10,12},{12... | collective-permute-start | bytes 442376 | tf_op jit(solution)/shard_map/ppermute | solution.py:42
  38.2 2.8 %collective-permute-start.10 = (f32[6,12,4,128]{3,2,1,0:T(4,128)S(1)}, f32[6,12,4,128]{3,2,1,0:T(4,128)S(1)}, u32[]{:S(2)}, u32[]{:S(2)}) collective-permute-start(f32[6,12,4,128]{3,2,1,0:T(4,128)S(1)} %get-tuple-element.158), channel_id=1, source_target_pairs={{2,0},{4,2},{6,4},{0,6},{3,1},{5,3},{7,5},{1,7},{10,8},{12,10},{14... | collective-permute-start | bytes 442376 | tf_op jit(solution)/shard_map/ppermute | solution.py:45
  42.1 3.6 %collective-permute-done.9 = f32[6,12,4,128]{3,2,1,0:T(4,128)S(1)} collective-permute-done((f32[6,12,4,128]{3,2,1,0:T(4,128)S(1)}, f32[6,12,4,128]{3,2,1,0:T(4,128)S(1)}, u32[]{:S(2)}, u32[]{:S(2)}) %collective-permute-start.9) | collective-permute-done | bytes 147488 | tf_op jit(solution)/shard_map/ppermute | solution.py:42
  45.7 1.1 %collective-permute-done.10 = f32[6,12,4,128]{3,2,1,0:T(4,128)S(1)} collective-permute-done((f32[6,12,4,128]{3,2,1,0:T(4,128)S(1)}, f32[6,12,4,128]{3,2,1,0:T(4,128)S(1)}, u32[]{:S(2)}, u32[]{:S(2)}) %collective-permute-start.10) | collective-permute-done | bytes 147488 | tf_op jit(solution)/shard_map/ppermute | solution.py:45
  47.1 1.1 %copy.411 = f32[6,12,16,4]{2,3,1,0:T(4,128)} copy(f32[6,12,16,4]{3,2,1,0:T(8,128)S(1)} %get-tuple-element.120) | data formatting | bytes 36864
  48.7 1.2 %copy.413 = f32[6,12,16,4]{2,3,1,0:T(4,128)} copy(f32[6,12,16,4]{3,2,1,0:T(8,128)S(1)} %get-tuple-element.121) | data formatting | bytes 36864
  50.4 0.7 copy.414
  51.0 0.7 copy.415
  53.3 0.7 pad_maximum_fusion
  54.1 1.5 %multiply_subtract_fusion = f32[4,10,14,134]{3,1,2,0:T(8,128)S(1)} fusion(f32[6,12,16,136]{3,1,2,0:T(8,128)S(1)} %pad_maximum_fusion), kind=kLoop, calls=%fused_computation.12 | loop fusion | flops 525280 | bytes 2401280 | tf_op jit(solution)/shard_map/sub | solution.py:55
  55.6 0.9 multiply_bitcast_fusion
  56.8 1.5 %subtract_multiply_fusion.3 = (f32[4,10,14,134]{3,1,2,0:T(8,128)S(1)}, f32[4,10,14,134]{3,1,2,0:T(8,128)S(1)}, f32[4,10,14,134]{3,1,2,0:T(8,128)S(1)}, f32[4,10,...) fusion(f32[6,12,16,136]{3,1,2,0:T(8,128)S(1)} %pad_maximum_fusion, ...), kind=kLoop, calls=%fused_computation.11 | loop fusion | flops 1800960 | bytes 4352320 | tf_op jit(solution)/shard_map/div | solution.py:89
  59.5 1.1 %slice.2153 = f32[6,10,14,128]{3,1,2,0:T(8,128)} slice(f32[6,10,14,134]{3,1,2,0:T(8,128)S(1)} %multiply_dynamic-update-slice_fusion), slice={[0:6], [0:10], [0:14], [3:131]} | slice | bytes 860160 | tf_op jit(solution)/shard_map/slice | solution.py:138
  60.6 1.5 %fusion.280 = (f32[6,10,14,1]{3,1,2,0:T(8,128)}, f32[6,10,14,1]{3,1,2,0:T(8,128)}) fusion(f32[6,10,14,134]{3,1,2,0:T(8,128)S(1)} %multiply_dynamic-update-slice_fusion), kind=kLoop, calls=%fused_computation.673 | loop fusion | bytes 13440 | tf_op jit(solution)/shard_map/slice | solution.py:139
  62.3 1.8 %copy.404 = f32[6,10,14,1]{1,2,0,3:T(8,128)S(1)} copy(f32[6,10,14,1]{3,1,2,0:T(8,128)} %get-tuple-element.98) | data formatting | bytes 6720 | tf_op jit(solution)/shard_map/broadcast_in_dim | solution.py:142
  64.0 2.4 %copy.405 = f32[6,10,14,1]{1,2,0,3:T(8,128)} copy(f32[6,10,14,1]{3,1,2,0:T(8,128)} %get-tuple-element.99) | data formatting | bytes 6720 | tf_op jit(solution)/shard_map/broadcast_in_dim | solution.py:145
  66.4 1.5 %slice_select_fusion.1 = (f32[6,10,14,3]{3,1,2,0:T(8,128)S(1)}, f32[6,10,14,3]{3,1,2,0:T(8,128)S(1)}) fusion(f32[6,10,14,134]{3,1,2,0:T(8,128)S(1)} %multiply_dynamic-update-slice_fusion, f32[6,10,14]{1,2,0:T(8,128)S(1)} %bitcast.158, pred[]{:T(512)S(6)} %eq.24, f32[6,10,14]{1,2,0:T(8,128)} %bitcast.159, pred[]{:T(512)S(6)} %eq.31), kind=kLoop, calls=%fused_computation.14 | loop fusion | flops 5040 | bytes 47042 | tf_op jit(solution)/shard_map/jit(_where)/select_n | solution.py:141
  68.7 0.9 fusion.27
  69.6 0.7 fusion.54
  71.3 0.6 copy.407
  75.7 1.3 %collective-permute-start.13 = (f32[6,4,8,8]{3,2,1,0:T(8,128)S(1)}, f32[6,4,8,8]{3,2,1,0:T(8,128)S(1)}, u32[]{:S(2)}, u32[]{:S(2)}) collective-permute-start(f32[6,4,8,8]{3,2,1,0:T(8,128)S(1)} %bitcast.149), channel_id=1, source_target_pairs={{1,0},{3,2},{5,4},{7,6},{9,8},{11,10},{13,12},{15,14},{17,16},{19,... | collective-permute-start | bytes 18440 | tf_op jit(solution)/shard_map/ppermute | solution.py:33
  79.0 1.3 %collective-permute-start.14 = (f32[6,2,8,128]{3,2,1,0:T(8,128)S(1)}, f32[6,2,8,128]{3,2,1,0:T(8,128)S(1)}, u32[]{:S(2)}, u32[]{:S(2)}) collective-permute-start(f32[6,2,8,128]{3,2,1,0:T(8,128)S(1)} %get-tuple-element.167), channel_id=1, source_target_pairs={{0,8},{8,16},{16,24},{24,0},{1,9},{9,17},{17,25},{25,1},{2,10},{10... | collective-permute-start | bytes 147464 | tf_op jit(solution)/shard_map/ppermute | solution.py:42
  80.4 1.6 %collective-permute-start.15 = (f32[6,2,8,128]{3,2,1,0:T(8,128)S(1)}, f32[6,2,8,128]{3,2,1,0:T(8,128)S(1)}, u32[]{:S(2)}, u32[]{:S(2)}) collective-permute-start(f32[6,2,8,128]{3,2,1,0:T(8,128)S(1)} %get-tuple-element.168), channel_id=1, source_target_pairs={{8,0},{16,8},{24,16},{0,24},{9,1},{17,9},{25,17},{1,25},{10,2},{18... | collective-permute-start | bytes 147464 | tf_op jit(solution)/shard_map/ppermute | solution.py:45
  82.0 2.4 %collective-permute-done.14 = f32[6,2,8,128]{3,2,1,0:T(8,128)S(1)} collective-permute-done((f32[6,2,8,128]{3,2,1,0:T(8,128)S(1)}, f32[6,2,8,128]{3,2,1,0:T(8,128)S(1)}, u32[]{:S(2)}, u32[]{:S(2)}) %collective-permute-start.14) | collective-permute-done | bytes 49184 | tf_op jit(solution)/shard_map/ppermute | solution.py:42
  84.5 1.1 %collective-permute-done.15 = f32[6,2,8,128]{3,2,1,0:T(8,128)S(1)} collective-permute-done((f32[6,2,8,128]{3,2,1,0:T(8,128)S(1)}, f32[6,2,8,128]{3,2,1,0:T(8,128)S(1)}, u32[]{:S(2)}, u32[]{:S(2)}) %collective-permute-start.15) | collective-permute-done | bytes 49184 | tf_op jit(solution)/shard_map/ppermute | solution.py:45
  85.6 1.6 %collective-permute-start.16 = (f32[6,8,2,128]{3,1,2,0:T(8,128)S(1)}, f32[6,8,2,128]{3,1,2,0:T(8,128)S(1)}, u32[]{:S(2)}, u32[]{:S(2)}) collective-permute-start(f32[6,8,2,128]{3,1,2,0:T(8,128)S(1)} %copy.426), channel_id=1, source_target_pairs={{0,2},{2,4},{4,6},{6,0},{1,3},{3,5},{5,7},{7,1},{8,10},{10,12},{12... | collective-permute-start | bytes 147464 | tf_op jit(solution)/shard_map/ppermute | solution.py:42
  87.3 2.2 %collective-permute-start.17 = (f32[6,8,2,128]{3,1,2,0:T(8,128)S(1)}, f32[6,8,2,128]{3,1,2,0:T(8,128)S(1)}, u32[]{:S(2)}, u32[]{:S(2)}) collective-permute-start(f32[6,8,2,128]{3,1,2,0:T(8,128)S(1)} %copy.427), channel_id=1, source_target_pairs={{2,0},{4,2},{6,4},{0,6},{3,1},{5,3},{7,5},{1,7},{10,8},{12,10},{14... | collective-permute-start | bytes 147464 | tf_op jit(solution)/shard_map/ppermute | solution.py:45
  89.5 2.4 %collective-permute-done.16 = f32[6,8,2,128]{3,1,2,0:T(8,128)S(1)} collective-permute-done((f32[6,8,2,128]{3,1,2,0:T(8,128)S(1)}, f32[6,8,2,128]{3,1,2,0:T(8,128)S(1)}, u32[]{:S(2)}, u32[]{:S(2)}) %collective-permute-start.16) | collective-permute-done | bytes 49184 | tf_op jit(solution)/shard_map/ppermute | solution.py:42
  93.6 0.6 copy.409
  97.0 0.6 copy.401
  (154 shorter events, 22.9 us)
Async XLA Ops:
  3.9 6.0 %collective-permute-start = (f32[6,2,8,128]{3,2,1,0:T(8,128)S(1)}, f32[6,2,8,128]{3,2,1,0:T(8,128)S(1)}, u32[]{:S(2)}, u32[]{:S(2)}) collective-permute-start(f32[6,2,8,128]{3,2,1,0:T(8,128)S(1)} %get-tuple-element.169), channel_id=1, source_target_pairs={{0,8},{8,16},{16,24},{24,0},{1,9},{9,17},{17,25},{25,1},{2,10},{10... | collective-permute-start | bytes 147464 | tf_op jit(solution)/shard_map/ppermute | solution.py:42
  6.9 4.1 %collective-permute-start.1 = (f32[6,2,8,128]{3,2,1,0:T(8,128)S(1)}, f32[6,2,8,128]{3,2,1,0:T(8,128)S(1)}, u32[]{:S(2)}, u32[]{:S(2)}) collective-permute-start(f32[6,2,8,128]{3,2,1,0:T(8,128)S(1)} %get-tuple-element.170), channel_id=1, source_target_pairs={{8,0},{16,8},{24,16},{0,24},{9,1},{17,9},{25,17},{1,25},{10,2},{18... | collective-permute-start | bytes 147464 | tf_op jit(solution)/shard_map/ppermute | solution.py:45
  11.8 6.0 %collective-permute-start.2 = (f32[6,8,2,128]{3,1,2,0:T(8,128)S(1)}, f32[6,8,2,128]{3,1,2,0:T(8,128)S(1)}, u32[]{:S(2)}, u32[]{:S(2)}) collective-permute-start(f32[6,8,2,128]{3,1,2,0:T(8,128)S(1)} %copy.424), channel_id=1, source_target_pairs={{0,2},{2,4},{4,6},{6,0},{1,3},{3,5},{5,7},{7,1},{8,10},{10,12},{12... | collective-permute-start | bytes 147464 | tf_op jit(solution)/shard_map/ppermute | solution.py:42
  13.5 4.7 %collective-permute-start.3 = (f32[6,8,2,128]{3,1,2,0:T(8,128)S(1)}, f32[6,8,2,128]{3,1,2,0:T(8,128)S(1)}, u32[]{:S(2)}, u32[]{:S(2)}) collective-permute-start(f32[6,8,2,128]{3,1,2,0:T(8,128)S(1)} %copy.425), channel_id=1, source_target_pairs={{2,0},{4,2},{6,4},{0,6},{3,1},{5,3},{7,5},{1,7},{10,8},{12,10},{14... | collective-permute-start | bytes 147464 | tf_op jit(solution)/shard_map/ppermute | solution.py:45
  18.3 2.0 %collective-permute-start.4 = (f32[6,8,12,2]{3,1,2,0:T(8,128)S(1)}, f32[6,8,12,2]{3,1,2,0:T(8,128)S(1)}, u32[]{:S(2)}, u32[]{:S(2)}) collective-permute-start(f32[6,8,12,2]{3,1,2,0:T(8,128)S(1)} %get-tuple-element.161), channel_id=1, source_target_pairs={{0,1},{1,0},{2,3},{3,2},{4,5},{5,4},{6,7},{7,6},{8,9},{9,8},{10,11... | collective-permute-start | bytes 13832 | tf_op jit(solution)/shard_map/ppermute | solution.py:42
  18.5 2.0 %collective-permute-start.5 = (f32[6,8,12,2]{3,1,2,0:T(8,128)S(1)}, f32[6,8,12,2]{3,1,2,0:T(8,128)S(1)}, u32[]{:S(2)}, u32[]{:S(2)}) collective-permute-start(f32[6,8,12,2]{3,1,2,0:T(8,128)S(1)} %get-tuple-element.162), channel_id=1, source_target_pairs={{1,0},{0,1},{3,2},{2,3},{5,4},{4,5},{7,6},{6,7},{9,8},{8,9},{11,10... | collective-permute-start | bytes 13832 | tf_op jit(solution)/shard_map/ppermute | solution.py:45
  23.2 2.2 %copy-start.6 = (s32[2]{0:T(128)S(1)}, s32[2]{0:T(128)}, u32[]{:S(2)}) copy-start(s32[2]{0:T(128)} %param.7) | copy-start | bytes 28
  23.2 4.8 %copy-start.1 = (f32[6,4,8,8]{3,2,1,0:T(8,128)S(1)}, f32[6,4,8,8]{3,2,1,0:T(8,128)}, u32[]{:S(2)}) copy-start(f32[6,4,8,8]{3,2,1,0:T(8,128)} %constant.63.clone.1) | copy-start | bytes 18436
  24.1 3.9 %collective-permute-start.6 = (f32[6,4,8,8]{3,2,1,0:T(8,128)S(1)}, f32[6,4,8,8]{3,2,1,0:T(8,128)S(1)}, u32[]{:S(2)}, u32[]{:S(2)}) collective-permute-start(f32[6,4,8,8]{3,2,1,0:T(8,128)S(1)} %bitcast.148), channel_id=1, source_target_pairs={{1,0},{3,2},{5,4},{7,6},{9,8},{11,10},{13,12},{15,14},{17,16},{19,... | collective-permute-start | bytes 18440 | tf_op jit(solution)/shard_map/ppermute | solution.py:33
  28.1 5.7 %collective-permute-start.8 = (f32[6,4,8,128]{3,2,1,0:T(8,128)S(1)}, f32[6,4,8,128]{3,2,1,0:T(8,128)S(1)}, u32[]{:S(2)}, u32[]{:S(2)}) collective-permute-start(f32[6,4,8,128]{3,2,1,0:T(8,128)S(1)} %fusion.19), channel_id=1, source_target_pairs={{8,0},{16,8},{24,16},{0,24},{9,1},{17,9},{25,17},{1,25},{10,2},{18... | collective-permute-start | bytes 294920 | tf_op jit(solution)/shard_map/ppermute | solution.py:45
  30.5 6.5 %collective-permute-start.7 = (f32[6,4,8,128]{3,2,1,0:T(8,128)S(1)}, f32[6,4,8,128]{3,2,1,0:T(8,128)S(1)}, u32[]{:S(2)}, u32[]{:S(2)}) collective-permute-start(f32[6,4,8,128]{3,2,1,0:T(8,128)S(1)} %fusion.19), channel_id=1, source_target_pairs={{0,8},{8,16},{16,24},{24,0},{1,9},{9,17},{17,25},{25,1},{2,10},{10... | collective-permute-start | bytes 294920 | tf_op jit(solution)/shard_map/ppermute | solution.py:42
  37.0 8.6 %collective-permute-start.9 = (f32[6,12,4,128]{3,2,1,0:T(4,128)S(1)}, f32[6,12,4,128]{3,2,1,0:T(4,128)S(1)}, u32[]{:S(2)}, u32[]{:S(2)}) collective-permute-start(f32[6,12,4,128]{3,2,1,0:T(4,128)S(1)} %get-tuple-element.157), channel_id=1, source_target_pairs={{0,2},{2,4},{4,6},{6,0},{1,3},{3,5},{5,7},{7,1},{8,10},{10,12},{12... | collective-permute-start | bytes 442376 | tf_op jit(solution)/shard_map/ppermute | solution.py:42
  38.2 8.6 %collective-permute-start.10 = (f32[6,12,4,128]{3,2,1,0:T(4,128)S(1)}, f32[6,12,4,128]{3,2,1,0:T(4,128)S(1)}, u32[]{:S(2)}, u32[]{:S(2)}) collective-permute-start(f32[6,12,4,128]{3,2,1,0:T(4,128)S(1)} %get-tuple-element.158), channel_id=1, source_target_pairs={{2,0},{4,2},{6,4},{0,6},{3,1},{5,3},{7,5},{1,7},{10,8},{12,10},{14... | collective-permute-start | bytes 442376 | tf_op jit(solution)/shard_map/ppermute | solution.py:45
  48.3 3.4 %collective-permute-start.11 = (f32[6,12,16,4]{2,3,1,0:T(4,128)}, f32[6,12,16,4]{2,3,1,0:T(4,128)S(1)}, u32[]{:S(2)}, u32[]{:S(2)}) collective-permute-start(f32[6,12,16,4]{2,3,1,0:T(4,128)} %copy.411), channel_id=1, source_target_pairs={{0,1},{1,0},{2,3},{3,2},{4,5},{5,4},{6,7},{7,6},{8,9},{9,8},{10,11... | collective-permute-start | bytes 55304 | tf_op jit(solution)/shard_map/ppermute | solution.py:42
  49.8 2.7 %collective-permute-start.12 = (f32[6,12,16,4]{2,3,1,0:T(4,128)}, f32[6,12,16,4]{2,3,1,0:T(4,128)S(1)}, u32[]{:S(2)}, u32[]{:S(2)}) collective-permute-start(f32[6,12,16,4]{2,3,1,0:T(4,128)} %copy.413), channel_id=1, source_target_pairs={{1,0},{0,1},{3,2},{2,3},{5,4},{4,5},{7,6},{6,7},{9,8},{8,9},{11,10... | collective-permute-start | bytes 55304 | tf_op jit(solution)/shard_map/ppermute | solution.py:45
  54.0 1.5 %copy-start.2 = (f32[134]{0:T(256)S(1)}, f32[134]{0:T(256)}, u32[]{:S(2)}) copy-start(f32[134]{0:T(256)} %get-tuple-element.181) | copy-start | bytes 1612
  54.0 1.5 %copy-start.3 = (f32[134]{0:T(256)S(1)}, f32[134]{0:T(256)}, u32[]{:S(2)}) copy-start(f32[134]{0:T(256)} %get-tuple-element.182) | copy-start | bytes 1612
  54.0 1.5 %copy-start.4 = (f32[134]{0:T(256)S(1)}, f32[134]{0:T(256)}, u32[]{:S(2)}) copy-start(f32[134]{0:T(256)} %get-tuple-element.183) | copy-start | bytes 1612
  54.0 1.5 %copy-start.5 = (f32[134]{0:T(256)S(1)}, f32[134]{0:T(256)}, u32[]{:S(2)}) copy-start(f32[134]{0:T(256)} %get-tuple-element.184) | copy-start | bytes 1612
  66.4 1.5 %copy-start = (f32[6,10,14,128]{3,1,2,0:T(8,128)S(1)}, f32[6,10,14,128]{3,1,2,0:T(8,128)}, u32[]{:S(2)}) copy-start(f32[6,10,14,128]{3,1,2,0:T(8,128)} %slice.2153) | copy-start | bytes 1290244
  75.7 3.2 %collective-permute-start.13 = (f32[6,4,8,8]{3,2,1,0:T(8,128)S(1)}, f32[6,4,8,8]{3,2,1,0:T(8,128)S(1)}, u32[]{:S(2)}, u32[]{:S(2)}) collective-permute-start(f32[6,4,8,8]{3,2,1,0:T(8,128)S(1)} %bitcast.149), channel_id=1, source_target_pairs={{1,0},{3,2},{5,4},{7,6},{9,8},{11,10},{13,12},{15,14},{17,16},{19,... | collective-permute-start | bytes 18440 | tf_op jit(solution)/shard_map/ppermute | solution.py:33
  79.0 5.4 %collective-permute-start.14 = (f32[6,2,8,128]{3,2,1,0:T(8,128)S(1)}, f32[6,2,8,128]{3,2,1,0:T(8,128)S(1)}, u32[]{:S(2)}, u32[]{:S(2)}) collective-permute-start(f32[6,2,8,128]{3,2,1,0:T(8,128)S(1)} %get-tuple-element.167), channel_id=1, source_target_pairs={{0,8},{8,16},{16,24},{24,0},{1,9},{9,17},{17,25},{25,1},{2,10},{10... | collective-permute-start | bytes 147464 | tf_op jit(solution)/shard_map/ppermute | solution.py:42
  80.4 5.2 %collective-permute-start.15 = (f32[6,2,8,128]{3,2,1,0:T(8,128)S(1)}, f32[6,2,8,128]{3,2,1,0:T(8,128)S(1)}, u32[]{:S(2)}, u32[]{:S(2)}) collective-permute-start(f32[6,2,8,128]{3,2,1,0:T(8,128)S(1)} %get-tuple-element.168), channel_id=1, source_target_pairs={{8,0},{16,8},{24,16},{0,24},{9,1},{17,9},{25,17},{1,25},{10,2},{18... | collective-permute-start | bytes 147464 | tf_op jit(solution)/shard_map/ppermute | solution.py:45
  85.6 6.3 %collective-permute-start.16 = (f32[6,8,2,128]{3,1,2,0:T(8,128)S(1)}, f32[6,8,2,128]{3,1,2,0:T(8,128)S(1)}, u32[]{:S(2)}, u32[]{:S(2)}) collective-permute-start(f32[6,8,2,128]{3,1,2,0:T(8,128)S(1)} %copy.426), channel_id=1, source_target_pairs={{0,2},{2,4},{4,6},{6,0},{1,3},{3,5},{5,7},{7,1},{8,10},{10,12},{12... | collective-permute-start | bytes 147464 | tf_op jit(solution)/shard_map/ppermute | solution.py:42
  87.3 4.7 %collective-permute-start.17 = (f32[6,8,2,128]{3,1,2,0:T(8,128)S(1)}, f32[6,8,2,128]{3,1,2,0:T(8,128)S(1)}, u32[]{:S(2)}, u32[]{:S(2)}) collective-permute-start(f32[6,8,2,128]{3,1,2,0:T(8,128)S(1)} %copy.427), channel_id=1, source_target_pairs={{2,0},{4,2},{6,4},{0,6},{3,1},{5,3},{7,5},{1,7},{10,8},{12,10},{14... | collective-permute-start | bytes 147464 | tf_op jit(solution)/shard_map/ppermute | solution.py:45
  92.2 2.0 %collective-permute-start.18 = (f32[6,8,12,2]{3,1,2,0:T(8,128)S(1)}, f32[6,8,12,2]{3,1,2,0:T(8,128)S(1)}, u32[]{:S(2)}, u32[]{:S(2)}) collective-permute-start(f32[6,8,12,2]{3,1,2,0:T(8,128)S(1)} %get-tuple-element.155), channel_id=1, source_target_pairs={{0,1},{1,0},{2,3},{3,2},{4,5},{5,4},{6,7},{7,6},{8,9},{9,8},{10,11... | collective-permute-start | bytes 13832 | tf_op jit(solution)/shard_map/ppermute | solution.py:42
  92.4 2.0 %collective-permute-start.19 = (f32[6,8,12,2]{3,1,2,0:T(8,128)S(1)}, f32[6,8,12,2]{3,1,2,0:T(8,128)S(1)}, u32[]{:S(2)}, u32[]{:S(2)}) collective-permute-start(f32[6,8,12,2]{3,1,2,0:T(8,128)S(1)} %get-tuple-element.156), channel_id=1, source_target_pairs={{1,0},{0,1},{3,2},{2,3},{5,4},{4,5},{7,6},{6,7},{9,8},{8,9},{11,10... | collective-permute-start | bytes 13832 | tf_op jit(solution)/shard_map/ppermute | solution.py:45
where the time goes:
time: 99.7 us; the launch traced here: 99.1 us
  other arithmetic  26.4 us (26%)
  starting transfers between devices  25.5 us (26%)
  waiting for transfers between devices  22.4 us (22%)
  local copies, waits for them, and re-layouts  19.4 us (19%)
  between operations  5.38 us (5%)
    ppermute x9, waiting for transfers between devices, with_halo(): lax.ppermute(lax.slice_in_dim(block, block.shape[dim] - width, None, axis...  15.7 us
    ppermute x9, starting transfers between devices, with_halo(): lax.ppermute(lax.slice_in_dim(block, 0, width, axis=dim), axis, backward)  13.9 us
    ppermute x9, starting transfers between devices, with_halo(): lax.ppermute(lax.slice_in_dim(block, block.shape[dim] - width, None, axis...  9.04 us
    ppermute x9, waiting for transfers between devices, with_halo(): lax.ppermute(lax.slice_in_dim(block, 0, width, axis=dim), axis, backward)  6.67 us
    broadcast_in_dim x5, local copies, waits for them, and re-layouts, clamp_ends(): jnp.broadcast_to(last_plane, block[..., -margin:].shape)  4.96 us
    broadcast_in_dim x5, local copies, waits for them, and re-layouts, clamp_ends(): jnp.broadcast_to(first_plane, block[..., :margin].shape)  4.29 us
    another operation x9, other arithmetic, potential_part(): return jnp.stack(results)  3.87 us
    unnamed x29, local copies, waits for them, and re-layouts  3.1 us
  transfers between devices with their start and end apart: 20, of which 11 were waited for; matrix products, arithmetic and copies ran while one was open for 9% of the time, Pallas kernels for 0%

commit v1 on v0

v1 whole, which is shorter than its diff:
```python
import functools
import math

import jax
import jax.numpy as jnp
from jax import lax
from jax.experimental import pallas as pl
from jax.experimental.pallas import tpu as pltpu
from jax.sharding import PartitionSpec as P

MESH = pl.DeviceIdType.MESH
STEPS = 4

interface_width = 4.0
time_step = 0.12
obstacle_coef = 16.0 / (math.pi * math.pi)
normal_floor = 0.25
surface_table = [
    [0.0, 1.0, 1.2, 0.9],
    [1.0, 0.0, 1.1, 1.0],
    [1.2, 1.1, 0.0, 0.8],
    [0.9, 1.0, 0.8, 0.0],
]
compositions = [[0.8, 0.1], [0.1, 0.8], [0.1, 0.1], [0.33, 0.33]]
latent_heat = [1.0, 0.9, 1.1, 0.0]
trapping_coef = math.pi * 4.0 / 4.0
undercool_span = 2.0

OWN, YH, ZH, YZ = 0, 1, 2, 3


def phase_update(center, nb, m, theta):
    lap = []
    for a in range(3):
        total = (nb[0][0][a] + nb[0][1][a]) + (nb[1][0][a] + nb[1][1][a])
        total = total + (nb[2][0][a] + nb[2][1][a])
        lap.append(total - 6.0 * center[a])
    lap.append(-(lap[0] + lap[1] + lap[2]))
    p = list(center) + [1.0 - (center[0] + center[1] + center[2])]

    def weigh(f, a):
        terms = [f[b] if surface_table[a][b] == 1.0 else surface_table[a][b] * f[b] for b in range(4) if b != a]
        return terms[0] + terms[1] + terms[2]

    drive = []
    for a in range(4):
        gp = weigh(p, a)
        gl = weigh(lap, a)
        v = gp * (obstacle_coef / interface_width - interface_width * lap[a]) + (interface_width * p[a]) * gl
        v = v - (compositions[a][0] * m[0] + compositions[a][1] * m[1])
        if latent_heat[a]:
            v = v + latent_heat[a] * theta
        drive.append(v)
    mean = 0.25 * ((drive[0] + drive[1]) + (drive[2] + drive[3]))
    q = [jnp.clip(p[a] - (time_step / interface_width) * (drive[a] - mean), 0.0, 1.0) for a in range(4)]
    inv = 1.0 / ((q[0] + q[1]) + (q[2] + q[3]))
    new = [q[a] * inv for a in range(4)]
    rate = [(new[a] - p[a]) * (1.0 / time_step) for a in range(4)]
    return p, new, rate


def carried_part(p, rate, nb):
    p3 = p[3] * 4.0
    carried, slopes = [], []
    for a in range(3):
        g = [0.5 * (nb[d][1][a] - nb[d][0][a]) for d in range(3)]
        square = g[0] * g[0] + g[1] * g[1] + g[2] * g[2]
        inv = lax.rsqrt(jnp.maximum(square, normal_floor * normal_floor))
        carried.append(p[a] * p3 * rate[a] * inv)
        slopes.append(g)
    return carried, slopes


def current(carried, slopes, d):
    out = []
    for k in range(2):
        total = None
        for a in range(3):
            term = (-trapping_coef * (compositions[3][k] - compositions[a][k])) * (carried[a] * slopes[a][d])
            total = term if total is None else total + term
        out.append(total)
    return out


def kernel(labels_ref, noise_ref, pot_ref, shift_ref, phase_out, pot_out,
           S, W, zrcv, ysnd, yrcv, csnd, crcv, send_sem, recv_sem):
    rows, ny, nl = noise_ref.shape[1:]
    gx, gy, gz = lax.axis_index("gx"), lax.axis_index("gy"), lax.axis_index("gz")
    nx_dev, ny_dev, nz_dev = lax.axis_size("gx"), lax.axis_size("gy"), lax.axis_size("gz")

    def near(index, count, step):
        return lax.rem(index + (count + step), count)

    xs = {-1: near(gx, nx_dev, -1), 1: near(gx, nx_dev, 1)}
    ys = {-1: near(gy, ny_dev, -1), 1: near(gy, ny_dev, 1)}
    zs = {-1: near(gz, nz_dev, -1), 1: near(gz, nz_dev, 1)}
    corners = [(-1, -1), (-1, 1), (1, -1), (1, 1)]
    targets = [{"gz": zs[-1]}, {"gz": zs[1]}, {"gx": xs[-1]}, {"gx": xs[1]}, {"gy": ys[-1]}, {"gy": ys[1]}]
    targets += [{"gx": xs[i], "gy": ys[j]} for i, j in corners]

    barrier = pltpu.get_barrier_semaphore()
    for target in targets:
        pl.semaphore_signal(barrier, inc=1, device_id=target, device_id_type=MESH)

    lane = lax.broadcasted_iota(jnp.int32, (ny, nl), 1)
    row = lax.broadcasted_iota(jnp.int32, (ny, nl), 0)
    lower = gz == 0
    upper = gz == nz_dev - 1
    total_planes = nl * nz_dev
    front = total_planes // 2
    zown = gz * nl + lane
    zhalo = jnp.where(lane < nl // 2, zown + nl, zown - nl)

    def theta_of(index):
        return undercool_span * (index.astype(jnp.float32) + 0.5 - front) / total_planes

    theta = {OWN: theta_of(zown), ZH: theta_of(zhalo)}
    theta[YH] = theta[OWN]
    solid = zown < front

    def up_y(a, b):
        return pltpu.roll(jnp.where(row == 0, b, a), ny - 1, 0)

    def down_y(a, b):
        return pltpu.roll(jnp.where(row == ny - 1, b, a), 1, 0)

    def up_z(a, b):
        return pltpu.roll(jnp.where(lane == 0, b, a), nl - 1, 1)

    def down_z(a, b):
        return pltpu.roll(jnp.where(lane == nl - 1, b, a), 1, 1)

    lrow = lax.broadcasted_iota(jnp.int32, (ny, ny), 0)
    lcol = lax.broadcasted_iota(jnp.int32, (ny, ny), 1)
    for x in range(rows):
        lab = jnp.broadcast_to(labels_ref[x : x + 1, :].astype(jnp.float32), (ny, ny))
        lab = jnp.sum(jnp.where(lrow == lcol, lab, 0.0), axis=1, keepdims=True)
        lab = jnp.broadcast_to(lab, (ny, nl))
        init = []
        for a in range(3):
            init.append(noise_ref[a, x] + jnp.where((lab == float(a)) & solid, 1.0, 0.0))
        init.append(noise_ref[3, x] + jnp.where(solid, 0.0, 1.0))
        inv = 1.0 / ((init[0] + init[1]) + (init[2] + init[3]))
        for a in range(3):
            S[0, a, x] = init[a] * inv
        for k in range(2):
            S[0, 3 + k, x] = pot_ref[k, x]

    pl.semaphore_wait(barrier, len(targets))

    def step(t, carry):
        def copy(src, dst, n, target):
            return pltpu.make_async_remote_copy(
                src_ref=src, dst_ref=dst, send_sem=send_sem.at[t, n], recv_sem=recv_sem.at[t, n],
                device_id=target, device_id_type=MESH,
            )

        zcopies = [
            copy(S.at[t], zrcv.at[t, 0], 0, {"gz": zs[1]}),
            copy(S.at[t], zrcv.at[t, 1], 1, {"gz": zs[-1]}),
        ]
        for c in zcopies:
            c.start()
        for c in zcopies:
            c.wait_recv()
        shift = shift_ref[t]
        bits = [(shift & 1) != 0, (shift & 2) != 0, (shift & 4) != 0, (shift & 8) != 0]
        for x in range(rows):
            for f in range(5):
                own = S[t, f, x]
                above = jnp.where(upper, 0.0, zrcv[t, 1, f, x])
                halo = jnp.where(lane < nl // 2, above, zrcv[t, 0, f, x])
                for bit in range(4):
                    by = 1 << bit
                    mixed_own = jnp.where(lane < by, halo, own)
                    mixed_halo = jnp.where(lane < by, own, halo)
                    own = jnp.where(bits[bit], pltpu.roll(mixed_own, nl - by, 1), own)
                    halo = jnp.where(bits[bit], pltpu.roll(mixed_halo, nl - by, 1), halo)
                first = jnp.broadcast_to(own[:, 0:1], (ny, nl))
                last = jnp.broadcast_to(own[:, nl - 1 : nl], (ny, nl))
                halo = jnp.where(upper & (lane < nl // 2), last, halo)
                halo = jnp.where(lower & (lane >= nl // 2), first, halo)
                W[t, f, x + 2, OWN] = own
                W[t, f, x + 2, ZH] = halo
                if f < 3:
                    ysnd[t, 0, f, 2 * x : 2 * x + 2, :] = own[0:2]
                    ysnd[t, 1, f, 2 * x : 2 * x + 2, :] = own[ny - 2 : ny]
                    at = f * rows + x
                    ysnd[t, 0, 4 + at // ny, at % ny : at % ny + 1, :] = halo[0:1]
                    ysnd[t, 1, 4 + at // ny, at % ny : at % ny + 1, :] = halo[ny - 1 : ny]
                    for n, (i, j) in enumerate(corners):
                        if x == (0 if i < 0 else rows - 1):
                            csnd[t, n, f : f + 1, :] = own[0:1] if j < 0 else own[ny - 1 : ny]
                else:
                    at = (f - 3) * rows + x
                    ysnd[t, 0, 3, at : at + 1, :] = own[0:1]
                    ysnd[t, 1, 3, at : at + 1, :] = own[ny - 1 : ny]

        copies = []
        for n, (i, j) in enumerate(corners):
            copies.append(copy(csnd.at[t, n], crcv.at[t, n], 2 + n, {"gx": xs[i], "gy": ys[j]}))
        low, high = (2, rows + 2), (rows, 0)
        for side, (src, dst) in ((-1, low), (1, high)):
            base = 6 + (0 if side < 0 else 3)
            edge_src = 2 if side < 0 else rows + 1
            edge_dst = rows + 2 if side < 0 else 1
            target = {"gx": xs[side]}
            copies.append(copy(W.at[t, pl.ds(0, 3), pl.ds(src, 2), OWN], W.at[t, pl.ds(0, 3), pl.ds(dst, 2), OWN], base, target))
            copies.append(copy(W.at[t, pl.ds(3, 2), edge_src, OWN], W.at[t, pl.ds(3, 2), edge_dst, OWN], base + 1, target))
            copies.append(copy(W.at[t, pl.ds(0, 3), edge_src, ZH], W.at[t, pl.ds(0, 3), edge_dst, ZH], base + 2, target))
        copies.append(copy(ysnd.at[t, 0], yrcv.at[t, 0], 12, {"gy": ys[-1]}))
        copies.append(copy(ysnd.at[t, 1], yrcv.at[t, 1], 13, {"gy": ys[1]}))
        for c in copies:
            c.start()
        for c in copies:
            c.wait_recv()

        for x in range(rows):
            for f in range(3):
                W[t, f, x + 2, YH, 0:2, :] = yrcv[t, 0, f, 2 * x : 2 * x + 2, :]
                W[t, f, x + 2, YH, ny - 2 : ny, :] = yrcv[t, 1, f, 2 * x : 2 * x + 2, :]
                at = f * rows + x
                W[t, f, x + 2, YZ, 0:1, :] = yrcv[t, 0, 4 + at // ny, at % ny : at % ny + 1, :]
                W[t, f, x + 2, YZ, ny - 1 : ny, :] = yrcv[t, 1, 4 + at // ny, at % ny : at % ny + 1, :]
            for k in range(2):
                at = k * rows + x
                W[t, 3 + k, x + 2, YH, 0:1, :] = yrcv[t, 0, 3, at : at + 1, :]
                W[t, 3 + k, x + 2, YH, ny - 1 : ny, :] = yrcv[t, 1, 3, at : at + 1, :]
        for n, (i, j) in enumerate(corners):
            xdst = rows + 2 if i < 0 else 1
            ydst = 0 if j < 0 else ny - 1
            for f in range(3):
                W[t, f, xdst, YH, ydst : ydst + 1, :] = crcv[t, n, f : f + 1, :]

        def field(x, q, fs=(0, 1, 2)):
            return [W[t, f, x, q] for f in fs]

        partner_y = {OWN: YH, YH: OWN, ZH: YZ}
        partner_z = {OWN: ZH, ZH: OWN, YH: YZ}

        def neighbours(x, q, fs=(0, 1, 2), with_x=True):
            c = field(x, q, fs)
            py = field(x, partner_y[q], fs)
            pz = field(x, partner_z[q], fs)
            n = len(fs)
            return c, [
                (field(x - 1, q, fs), field(x + 1, q, fs)),
                ([down_y(c[a], py[a]) for a in range(n)], [up_y(c[a], py[a]) for a in range(n)]),
                ([down_z(c[a], pz[a]) for a in range(n)], [up_z(c[a], pz[a]) for a in range(n)]),
            ]

        jx = {}
        partial = {}
        for x in range(1, rows + 3):
            inside = 2 <= x < rows + 2
            m = field(x, OWN, (3, 4))
            c, nb = neighbours(x, OWN)
            p, new, rate = phase_update(c, nb, m, theta[OWN])
            carried, slopes = carried_part(p, rate, nb)
            jx[x] = current(carried, slopes, 0)
            if inside:
                for a in range(3):
                    S[t + 1, a, x - 2] = new[a]
                phase_out[3, x - 2] = new[3]
                _, mb = neighbours(x, OWN, (3, 4))
                diff = [None, None]
                s = (c[0] + c[1]) + c[2]
                for d in range(3):
                    for side in range(2):
                        around = nb[d][side]
                        mob = 1.0 - 0.45 * (((around[0] + around[1]) + around[2]) + s)
                        for k in range(2):
                            flow = mob * (mb[d][side][k] - m[k])
                            diff[k] = flow if diff[k] is None else diff[k] + flow
                for k in range(2):
                    for a in range(4):
                        diff[k] = diff[k] - compositions[a][k] * rate[a]
                jy = current(carried, slopes, 1)
                jz = current(carried, slopes, 2)
                cb, nbb = neighbours(x, YH)
                pb, _, rb = phase_update(cb, nbb, field(x, YH, (3, 4)), theta[YH])
                jyb = current(*carried_part(pb, rb, nbb), 1)
                cz, nbz = neighbours(x, ZH)
                pz, _, rz = phase_update(cz, nbz, field(x, ZH, (3, 4)), theta[ZH])
                jzb = current(*carried_part(pz, rz, nbz), 2)
                for k in range(2):
                    dy = up_y(jy[k], jyb[k]) - down_y(jy[k], jyb[k])
                    above = jnp.where(upper & (lane == nl - 1), jz[k], up_z(jz[k], jzb[k]))
                    below = jnp.where(lower & (lane == 0), jz[k], down_z(jz[k], jzb[k]))
                    diff[k] = diff[k] - 0.5 * (dy + (above - below))
                partial[x] = (m, diff)
            if x >= 3:
                at = x - 1
                if 2 <= at < rows + 2:
                    m_at, diff_at = partial.pop(at)
                    for k in range(2):
                        total = diff_at[k] - 0.5 * (jx[at + 1][k] - jx[at - 1][k])
                        S[t + 1, 3 + k, at - 2] = m_at[k] + time_step * total
        for c in zcopies + copies:
            c.wait_send()
        return carry

    lax.fori_loop(0, STEPS, step, 0)
    for a in range(3):
        phase_out[a] = S[STEPS, a]
    for k in range(2):
        pot_out[k] = S[STEPS, 3 + k]


def on_device(labels, phase_noise, potentials, frame_shift):
    _, rows, ny, nl = phase_noise.shape
    none = jnp.zeros((1,), jnp.int32)
    shifts = jnp.concatenate([none, frame_shift[0:1], none, frame_shift[1:2]])
    shifts = jnp.broadcast_to(shifts[:, None, None], (STEPS, ny, nl))
    vmem = pl.BlockSpec(memory_space=pltpu.VMEM)
    f32 = jnp.float32
    return pl.pallas_call(
        kernel,
        out_shape=(
            jax.ShapeDtypeStruct(phase_noise.shape, f32),
            jax.ShapeDtypeStruct(potentials.shape, f32),
        ),
        in_specs=[vmem] * 4,
        out_specs=(vmem, vmem),
        scratch_shapes=[
            pltpu.VMEM((STEPS + 1, 5, rows, ny, nl), f32),
            pltpu.VMEM((STEPS, 5, rows + 4, 4, ny, nl), f32),
            pltpu.VMEM((STEPS, 2, 5, rows, ny, nl), f32),
            pltpu.VMEM((STEPS, 2, 6, ny, nl), f32),
            pltpu.VMEM((STEPS, 2, 6, ny, nl), f32),
            pltpu.VMEM((STEPS, 4, ny, nl), f32),
            pltpu.VMEM((STEPS, 4, ny, nl), f32),
            pltpu.SemaphoreType.DMA((STEPS, 14)),
            pltpu.SemaphoreType.DMA((STEPS, 14)),
        ],
        compiler_params=pltpu.CompilerParams(collective_id=0, has_side_effects=True),
        name="eutectic",
    )(labels, phase_noise, potentials, shifts)


def solution(mesh):
    placed = (P("gx", "gy"), P(None, "gx", "gy", "gz"), P(None, "gx", "gy", "gz"), P())
    return jax.shard_map(
        on_device,
        mesh=mesh,
        in_specs=placed,
        out_specs=(P(None, "gx", "gy", "gz"), P(None, "gx", "gy", "gz")),
        check_vma=False,
    )
```

time: 99.7 us -> 41.7 us (0.42)
  Pallas kernels: 0 us -> 35.3 us
  starting transfers between devices: 25.5 us -> 0 us
  other arithmetic: 26.4 us -> 1.37 us
  waiting for transfers between devices: 22.4 us -> 0 us
  local copies, waits for them, and re-layouts: 19.4 us -> 4.09 us
  between operations: 5.38 us -> 0.65 us
    pallas_call x0 -> x1, Pallas kernels: none -> 35.3 us  [on_device(): pl.pallas_call(kernel, out_shape=(jax.ShapeDtypeStruct(phase_noise.shape,...]
    ppermute x20 -> x0, starting transfers between devices: 25.5 us -> none  [the longest x9 13.9 us: with_halo(): lax.ppermute(lax.slice_in_dim(block, 0, width, axis=dim), axis, backward)]
    ppermute x20 -> x0, waiting for transfers between devices: 22.4 us -> none  [the longest x9 15.7 us: with_halo(): lax.ppermute(lax.slice_in_dim(block, block.shape[dim] - width, None, axis...]
    broadcast_in_dim x10 -> x1, local copies, waits for them, and re-layouts: 9.25 us -> 0.68 us  [on_device(): shifts = jnp.broadcast_to(shifts[:, None, None], (STEPS, ny, nl))]
    div x8 -> x0, other arithmetic: 4.69 us -> none  [the longest x4 2.01 us: phase_part(): change = (updated - interior) / time_step]
    slice x22 -> x1, local copies, waits for them, and re-layouts: 5.54 us -> 1.31 us  [on_device(): shifts = jnp.concatenate([none, frame_shift[0:1], none, frame_shift[1:2]])]
    another operation x13 -> x0, other arithmetic: 4.15 us -> none  [the longest x9 3.87 us: potential_part(): return jnp.stack(results)]
    concatenate x16 -> x1, other arithmetic: 4.91 us -> 1.37 us  [on_device(): shifts = jnp.concatenate([none, frame_shift[0:1], none, frame_shift[1:2]])]
  transfers between devices with their start and end apart: 20 -> 0, of which waited for: 11 -> 0; matrix products, arithmetic and copies ran while one was open for 9% -> 0% of each run, Pallas kernels for 0% -> 0%
where the time goes in v1:
time: 41.7 us; the launch traced here: 41.4 us
  Pallas kernels  35.3 us (85%)
  local copies, waits for them, and re-layouts  4.09 us (10%)
  other arithmetic  1.37 us (3%)
  between operations  0.65 us (2%)
    pallas_call x1, Pallas kernels, on_device(): pl.pallas_call(kernel, out_shape=(jax.ShapeDtypeStruct(phase_noise.shape,...  35.3 us
    unnamed x4, local copies, waits for them, and re-layouts  2.1 us
    concatenate x1, other arithmetic, on_device(): shifts = jnp.concatenate([none, frame_shift[0:1], none, frame_shift[1:2]])  1.37 us
    slice x1, local copies, waits for them, and re-layouts, on_device(): shifts = jnp.concatenate([none, frame_shift[0:1], none, frame_shift[1:2]])  1.31 us

profile of v1, /device:TPU:0, one launch (start us, length us, event | category | flops | bytes accessed | tf_op | source)
XLA Modules:
  0.0 41.4 jit_solution(18322244005792344507)
XLA Ops:
  0.6 1.3 %fusion = (s32[1]{0:T(128)}, s32[1]{0:T(128)}) fusion(s32[2]{0:T(128)} %param.7), kind=kLoop, calls=%fused_computation.1 | loop fusion | bytes 16 | tf_op jit(solution)/shard_map/slice | solution.py:313
  1.9 1.4 %pad_add_fusion = s32[4]{0:T(128)S(1)} fusion(s32[1]{0:T(128)} %get-tuple-element.3, s32[1]{0:T(128)} %constant.0.clone.1, s32[1]{0:T(128)} %get-tuple-element.2), kind=kLoop, calls=%fused_computation | loop fusion | flops 12 | bytes 28 | tf_op jit(solution)/shard_map/concatenate | solution.py:313
  3.3 0.7 %broadcast_in_dim.2.shift_ref = s32[4,8,128]{2,1,0:T(8,128)} broadcast(s32[4]{0:T(128)S(1)} %pad_add_fusion), dimensions={0} | broadcast | bytes 16400 | tf_op jit(solution)/shard_map/broadcast_in_dim | solution.py:314
  4.0 35.3 %eutectic.1 = (f32[4,4,8,128]{3,2,1,0:T(8,128)}, f32[2,4,8,128]{3,2,1,0:T(8,128)}) custom-call(s32[4,8]{1,0:T(4,128)} %labels_ref.1, f32[4,4,8,128]{3,2,1,0:T(8,128)} %noise_ref.1, f32[2,4,8,128]{3,2,1,0:T(8,128)} %pot_ref.1, s32[4,8,128]{2,1,0:T(8,128)} %broadcast_in_dim.2.shift_ref), custom_call_target="tpu_custom_call" | custom-call | tf_op jit(solution)/shard_map/eutectic/pallas_call | solution.py:317
  39.3 0.0 copy-start
  39.3 1.5 %copy.8 = f32[4,4,8,128]{3,2,1,0:T(8,128)} copy(f32[4,4,8,128]{3,2,1,0:T(8,128)} %get-tuple-element.6) | data formatting | bytes 131072
  40.8 0.0 copy-done
  40.8 0.6 %copy.9 = f32[2,4,8,128]{3,2,1,0:T(8,128)} copy(f32[2,4,8,128]{3,2,1,0:T(8,128)S(1)} %copy-done) | data formatting | bytes 65536
Async XLA Ops:
  39.3 1.5 %copy-start = (f32[2,4,8,128]{3,2,1,0:T(8,128)S(1)}, f32[2,4,8,128]{3,2,1,0:T(8,128)}, u32[]{:S(2)}) copy-start(f32[2,4,8,128]{3,2,1,0:T(8,128)} %get-tuple-element.7) | copy-start | bytes 98308

commit v2 on v1

--- a/solution.py
+++ b/solution.py
@@ -82,8 +82,17 @@
     return out
 
 
-def kernel(labels_ref, noise_ref, pot_ref, shift_ref, phase_out, pot_out,
-           S, W, zrcv, ysnd, yrcv, csnd, crcv, send_sem, recv_sem):
+def kernel(labels_hbm, noise_hbm, pot_hbm, shift_hbm, phase_out, pot_out,
+           labels_ref, noise_ref, pot_ref, shift_ref, in_sem,
+           S, W, zrcv, ysnd, yrcv, yzsnd, yzrcv, xzsnd, xzrcv, csnd, crcv, send_sem, recv_sem):
+    fetches = [
+        pltpu.make_async_copy(src, dst, in_sem.at[n])
+        for n, (src, dst) in enumerate(
+            ((labels_hbm, labels_ref), (noise_hbm, noise_ref), (pot_hbm, pot_ref), (shift_hbm, shift_ref))
+        )
+    ]
+    for fetch in fetches:
+        fetch.start()
     rows, ny, nl = noise_ref.shape[1:]
     gx, gy, gz = lax.axis_index("gx"), lax.axis_index("gy"), lax.axis_index("gz")
     nx_dev, ny_dev, nz_dev = lax.axis_size("gx"), lax.axis_size("gy"), lax.axis_size("gz")
@@ -95,8 +104,8 @@
     ys = {-1: near(gy, ny_dev, -1), 1: near(gy, ny_dev, 1)}
     zs = {-1: near(gz, nz_dev, -1), 1: near(gz, nz_dev, 1)}
     corners = [(-1, -1), (-1, 1), (1, -1), (1, 1)]
-    targets = [{"gz": zs[-1]}, {"gz": zs[1]}, {"gx": xs[-1]}, {"gx": xs[1]}, {"gy": ys[-1]}, {"gy": ys[1]}]
-    targets += [{"gx": xs[i], "gy": ys[j]} for i, j in corners]
+    targets = [{"gx": xs[i], "gy": ys[j]} for i, j in corners]
+    targets += [{"gx": xs[-1]}, {"gx": xs[1]}, {"gy": ys[-1]}, {"gy": ys[1]}, {"gz": zs[-1]}, {"gz": zs[1]}]
 
     barrier = pltpu.get_barrier_semaphore()
     for target in targets:
@@ -130,6 +139,9 @@
     def down_z(a, b):
         return pltpu.roll(jnp.where(lane == nl - 1, b, a), 1, 1)
 
+    for fetch in fetches:
+        fetch.wait()
+    first_shift, second_shift = shift_ref[0], shift_ref[1]
     lrow = lax.broadcasted_iota(jnp.int32, (ny, ny), 0)
     lcol = lax.broadcasted_iota(jnp.int32, (ny, ny), 1)
     for x in range(rows):
@@ -142,86 +154,124 @@
         init.append(noise_ref[3, x] + jnp.where(solid, 0.0, 1.0))
         inv = 1.0 / ((init[0] + init[1]) + (init[2] + init[3]))
         for a in range(3):
-            S[0, a, x] = init[a] * inv
+            W[0, a, x + 2, OWN] = init[a] * inv
         for k in range(2):
-            S[0, 3 + k, x] = pot_ref[k, x]
+            W[0, 3 + k, x + 2, OWN] = pot_ref[k, x]
 
     pl.semaphore_wait(barrier, len(targets))
 
-    def step(t, carry):
+    def step(t, shifted, store):
         def copy(src, dst, n, target):
             return pltpu.make_async_remote_copy(
                 src_ref=src, dst_ref=dst, send_sem=send_sem.at[t, n], recv_sem=recv_sem.at[t, n],
                 device_id=target, device_id_type=MESH,
             )
 
+        block = S.at[t // 2] if shifted else W.at[t, pl.ds(0, 5), pl.ds(2, rows), OWN]
         zcopies = [
-            copy(S.at[t], zrcv.at[t, 0], 0, {"gz": zs[1]}),
-            copy(S.at[t], zrcv.at[t, 1], 1, {"gz": zs[-1]}),
+            copy(block, zrcv.at[t, 0], 0, {"gz": zs[1]}),
+            copy(block, zrcv.at[t, 1], 1, {"gz": zs[-1]}),
         ]
         for c in zcopies:
             c.start()
+
+        copies = []
+
+        def launch(c):
+            c.start()
+            copies.append(c)
+
+        def pack_own(x, f, own):
+            if f < 3:
+                ysnd[t, 0, f, 2 * x : 2 * x + 2, :] = own[0:2]
+                ysnd[t, 1, f, 2 * x : 2 * x + 2, :] = own[ny - 2 : ny]
+                for n, (i, j) in enumerate(corners):
+                    if x == (0 if i < 0 else rows - 1):
+                        csnd[t, n, f : f + 1, :] = own[0:1] if j < 0 else own[ny - 1 : ny]
+            else:
+                at = (f - 3) * rows + x
+                ysnd[t, 0, 3, at : at + 1, :] = own[0:1]
+                ysnd[t, 1, 3, at : at + 1, :] = own[ny - 1 : ny]
+
+        def send_own():
+            low, high = (2, rows + 2), (rows, 0)
+            for side, (src, dst) in ((-1, low), (1, high)):
+                base = 6 + (0 if side < 0 else 2)
+                edge_src = 2 if side < 0 else rows + 1
+                edge_dst = rows + 2 if side < 0 else 1
+                target = {"gx": xs[side]}
+                launch(copy(W.at[t, pl.ds(0, 3), pl.ds(src, 2), OWN], W.at[t, pl.ds(0, 3), pl.ds(dst, 2), OWN], base, target))
+                launch(copy(W.at[t, pl.ds(3, 2), edge_src, OWN], W.at[t, pl.ds(3, 2), edge_dst, OWN], base + 1, target))
+
+        def send_y():
+            for n, (i, j) in enumerate(corners):
+                launch(copy(csnd.at[t, n], crcv.at[t, n], 2 + n, {"gx": xs[i], "gy": ys[j]}))
+            launch(copy(ysnd.at[t, 0], yrcv.at[t, 0], 10, {"gy": ys[-1]}))
+            launch(copy(ysnd.at[t, 1], yrcv.at[t, 1], 11, {"gy": ys[1]}))
+
+        if not shifted:
+            send_own()
+            for x in range(rows):
+                for f in range(5):
+                    pack_own(x, f, W[t, f, x + 2, OWN])
+            send_y()
         for c in zcopies:
             c.wait_recv()
-        shift = shift_ref[t]
-        bits = [(shift & 1) != 0, (shift & 2) != 0, (shift & 4) != 0, (shift & 8) != 0]
+        if shifted:
+            shift = jnp.full((ny, nl), jnp.where(t == 1, first_shift, second_shift), jnp.int32)
+            bits = [(shift & 1) != 0, (shift & 2) != 0, (shift & 4) != 0, (shift & 8) != 0]
+        packed = {}
         for x in range(rows):
             for f in range(5):
-                own = S[t, f, x]
-                above = jnp.where(upper, 0.0, zrcv[t, 1, f, x])
-                halo = jnp.where(lane < nl // 2, above, zrcv[t, 0, f, x])
-                for bit in range(4):
-                    by = 1 << bit
-                    mixed_own = jnp.where(lane < by, halo, own)
-                    mixed_halo = jnp.where(lane < by, own, halo)
-                    own = jnp.where(bits[bit], pltpu.roll(mixed_own, nl - by, 1), own)
-                    halo = jnp.where(bits[bit], pltpu.roll(mixed_halo, nl - by, 1), halo)
+                own = S[t // 2, f, x] if shifted else W[t, f, x + 2, OWN]
+                halo = jnp.where(lane < nl // 2, zrcv[t, 1, f, x], zrcv[t, 0, f, x])
+                if shifted:
+                    halo = jnp.where(upper & (lane < nl // 2), 0.0, halo)
+                    for bit in range(4):
+                        by = 1 << bit
+                        mixed_own = jnp.where(lane < by, halo, own)
+                        mixed_halo = jnp.where(lane < by, own, halo)
+                        own = jnp.where(bits[bit], pltpu.roll(mixed_own, nl - by, 1), own)
+                        halo = jnp.where(bits[bit], pltpu.roll(mixed_halo, nl - by, 1), halo)
+                    W[t, f, x + 2, OWN] = own
+                    pack_own(x, f, own)
                 first = jnp.broadcast_to(own[:, 0:1], (ny, nl))
                 last = jnp.broadcast_to(own[:, nl - 1 : nl], (ny, nl))
                 halo = jnp.where(upper & (lane < nl // 2), last, halo)
                 halo = jnp.where(lower & (lane >= nl // 2), first, halo)
-                W[t, f, x + 2, OWN] = own
                 W[t, f, x + 2, ZH] = halo
                 if f < 3:
-                    ysnd[t, 0, f, 2 * x : 2 * x + 2, :] = own[0:2]
-                    ysnd[t, 1, f, 2 * x : 2 * x + 2, :] = own[ny - 2 : ny]
                     at = f * rows + x
-                    ysnd[t, 0, 4 + at // ny, at % ny : at % ny + 1, :] = halo[0:1]
-                    ysnd[t, 1, 4 + at // ny, at % ny : at % ny + 1, :] = halo[ny - 1 : ny]
-                    for n, (i, j) in enumerate(corners):
-                        if x == (0 if i < 0 else rows - 1):
-                            csnd[t, n, f : f + 1, :] = own[0:1] if j < 0 else own[ny - 1 : ny]
-                else:
-                    at = (f - 3) * rows + x
-                    ysnd[t, 0, 3, at : at + 1, :] = own[0:1]
-                    ysnd[t, 1, 3, at : at + 1, :] = own[ny - 1 : ny]
-
-        copies = []
-        for n, (i, j) in enumerate(corners):
-            copies.append(copy(csnd.at[t, n], crcv.at[t, n], 2 + n, {"gx": xs[i], "gy": ys[j]}))
-        low, high = (2, rows + 2), (rows, 0)
-        for side, (src, dst) in ((-1, low), (1, high)):
-            base = 6 + (0 if side < 0 else 3)
-            edge_src = 2 if side < 0 else rows + 1
-            edge_dst = rows + 2 if side < 0 else 1
-            target = {"gx": xs[side]}
-            copies.append(copy(W.at[t, pl.ds(0, 3), pl.ds(src, 2), OWN], W.at[t, pl.ds(0, 3), pl.ds(dst, 2), OWN], base, target))
-            copies.append(copy(W.at[t, pl.ds(3, 2), edge_src, OWN], W.at[t, pl.ds(3, 2), edge_dst, OWN], base + 1, target))
-            copies.append(copy(W.at[t, pl.ds(0, 3), edge_src, ZH], W.at[t, pl.ds(0, 3), edge_dst, ZH], base + 2, target))
-        copies.append(copy(ysnd.at[t, 0], yrcv.at[t, 0], 12, {"gy": ys[-1]}))
-        copies.append(copy(ysnd.at[t, 1], yrcv.at[t, 1], 13, {"gy": ys[1]}))
-        for c in copies:
-            c.start()
+                    yzsnd[t, 0, at // ny, at % ny : at % ny + 1, :] = halo[0:1]
+                    yzsnd[t, 1, at // ny, at % ny : at % ny + 1, :] = halo[ny - 1 : ny]
+                    if x == 0 or x == rows - 1:
+                        mixed = halo if f == 0 else jnp.where(
+                            (lane == 8 * f) | (lane == 8 * f - 1), pltpu.roll(halo, 8 * f, 1), packed[x])
+                        packed[x] = mixed
+        xzsnd[t, 0] = packed[0]
+        xzsnd[t, 1] = packed[rows - 1]
+        if shifted:
+            send_own()
+            send_y()
+        launch(copy(xzsnd.at[t, 0], xzrcv.at[t, 0], 12, {"gx": xs[-1]}))
+        launch(copy(xzsnd.at[t, 1], xzrcv.at[t, 1], 13, {"gx": xs[1]}))
+        launch(copy(yzsnd.at[t, 0], yzrcv.at[t, 0], 14, {"gy": ys[-1]}))
+        launch(copy(yzsnd.at[t, 1], yzrcv.at[t, 1], 15, {"gy": ys[1]}))
         for c in copies:
             c.wait_recv()
 
+        for f in range(3):
+            by = 8 * f
+            for slot, xdst in ((0, rows + 2), (1, 1)):
+                halo = xzrcv[t, slot]
+                W[t, f, xdst, ZH] = pltpu.roll(halo, nl - by, 1) if by else halo
         for x in range(rows):
             for f in range(3):
                 W[t, f, x + 2, YH, 0:2, :] = yrcv[t, 0, f, 2 * x : 2 * x + 2, :]
                 W[t, f, x + 2, YH, ny - 2 : ny, :] = yrcv[t, 1, f, 2 * x : 2 * x + 2, :]
                 at = f * rows + x
-                W[t, f, x + 2, YZ, 0:1, :] = yrcv[t, 0, 4 + at // ny, at % ny : at % ny + 1, :]
-                W[t, f, x + 2, YZ, ny - 1 : ny, :] = yrcv[t, 1, 4 + at // ny, at % ny : at % ny + 1, :]
+                W[t, f, x + 2, YZ, 0:1, :] = yzrcv[t, 0, at // ny, at % ny : at % ny + 1, :]
+                W[t, f, x + 2, YZ, ny - 1 : ny, :] = yzrcv[t, 1, at // ny, at % ny : at % ny + 1, :]
             for k in range(2):
                 at = k * rows + x
                 W[t, 3 + k, x + 2, YH, 0:1, :] = yrcv[t, 0, 3, at : at + 1, :]
@@ -260,7 +310,7 @@
             jx[x] = current(carried, slopes, 0)
             if inside:
                 for a in range(3):
-                    S[t + 1, a, x - 2] = new[a]
+                    store(a, x - 2, new[a])
                 phase_out[3, x - 2] = new[3]
                 _, mb = neighbours(x, OWN, (3, 4))
                 diff = [None, None]
@@ -295,47 +345,68 @@
                     m_at, diff_at = partial.pop(at)
                     for k in range(2):
                         total = diff_at[k] - 0.5 * (jx[at + 1][k] - jx[at - 1][k])
-                        S[t + 1, 3 + k, at - 2] = m_at[k] + time_step * total
+                        store(3 + k, at - 2, m_at[k] + time_step * total)
         for c in zcopies + copies:
             c.wait_send()
+
+    def pair(tt, carry):
+        def to_block(f, x, value):
+            S[tt, f, x] = value
+
+        def to_window(f, x, value):
+            W[2 * tt + 2, f, x + 2, OWN] = value
+
+        step(2 * tt, False, to_block)
+        step(2 * tt + 1, True, to_window)
         return carry
 
-    lax.fori_loop(0, STEPS, step, 0)
-    for a in range(3):
-        phase_out[a] = S[STEPS, a]
-    for k in range(2):
-        pot_out[k] = S[STEPS, 3 + k]
+    lax.fori_loop(0, STEPS // 2, pair, 0)
+    for x in range(rows):
+        for a in range(3):
+            phase_out[a, x] = W[STEPS, a, x + 2, OWN]
+        for k in range(2):
+            pot_out[k, x] = W[STEPS, 3 + k, x + 2, OWN]
 
 
 def on_device(labels, phase_noise, potentials, frame_shift):
     _, rows, ny, nl = phase_noise.shape
-    none = jnp.zeros((1,), jnp.int32)
-    shifts = jnp.concatenate([none, frame_shift[0:1], none, frame_shift[1:2]])
-    shifts = jnp.broadcast_to(shifts[:, None, None], (STEPS, ny, nl))
     vmem = pl.BlockSpec(memory_space=pltpu.VMEM)
+    hbm = pl.BlockSpec(memory_space=pltpu.HBM)
     f32 = jnp.float32
+    zrows = -(-3 * rows // ny)
     return pl.pallas_call(
         kernel,
         out_shape=(
             jax.ShapeDtypeStruct(phase_noise.shape, f32),
             jax.ShapeDtypeStruct(potentials.shape, f32),
         ),
-        in_specs=[vmem] * 4,
+        in_specs=[hbm] * 4,
         out_specs=(vmem, vmem),
         scratch_shapes=[
-            pltpu.VMEM((STEPS + 1, 5, rows, ny, nl), f32),
-            pltpu.VMEM((STEPS, 5, rows + 4, 4, ny, nl), f32),
+            pltpu.VMEM(labels.shape, jnp.int32),
+            pltpu.VMEM(phase_noise.shape, f32),
+            pltpu.VMEM(potentials.shape, f32),
+            pltpu.SMEM(frame_shift.shape, jnp.int32),
+            pltpu.SemaphoreType.DMA((4,)),
+            pltpu.VMEM((STEPS // 2, 5, rows, ny, nl), f32),
+            pltpu.VMEM((STEPS + 1, 5, rows + 4, 4, ny, nl), f32),
             pltpu.VMEM((STEPS, 2, 5, rows, ny, nl), f32),
-            pltpu.VMEM((STEPS, 2, 6, ny, nl), f32),
-            pltpu.VMEM((STEPS, 2, 6, ny, nl), f32),
+            pltpu.VMEM((STEPS, 2, 4, ny, nl), f32),
+            pltpu.VMEM((STEPS, 2, 4, ny, nl), f32),
+            pltpu.VMEM((STEPS, 2, zrows, ny, nl), f32),
+            pltpu.VMEM((STEPS, 2, zrows, ny, nl), f32),
+            pltpu.VMEM((STEPS, 2, ny, nl), f32),
+            pltpu.VMEM((STEPS, 2, ny, nl), f32),
             pltpu.VMEM((STEPS, 4, ny, nl), f32),
             pltpu.VMEM((STEPS, 4, ny, nl), f32),
-            pltpu.SemaphoreType.DMA((STEPS, 14)),
-            pltpu.SemaphoreType.DMA((STEPS, 14)),
+            pltpu.SemaphoreType.DMA((STEPS, 16)),
+            pltpu.SemaphoreType.DMA((STEPS, 16)),
         ],
-        compiler_params=pltpu.CompilerParams(collective_id=0, has_side_effects=True),
+        compiler_params=pltpu.CompilerParams(
+            collective_id=0, has_side_effects=True, vmem_limit_bytes=16 * 1024 * 1024
+        ),
         name="eutectic",
-    )(labels, phase_noise, potentials, shifts)
+    )(labels, phase_noise, potentials, frame_shift)
 
 
 def solution(mesh):

time: 41.7 us -> 36.3 us (0.87)
  Pallas kernels: 35.3 us -> 31.2 us
  other arithmetic: 1.37 us -> 0 us
    pallas_call x1, Pallas kernels: 35.3 us -> 31.2 us  [on_device(): pl.pallas_call(kernel, out_shape=(jax.ShapeDtypeStruct(phase_noise.shape,...]
    unnamed x4 -> x10, local copies, waits for them, and re-layouts: 2.1 us -> 4.17 us
    concatenate x1 -> x0, other arithmetic: 1.37 us -> none  [on_device(): shifts = jnp.concatenate([none, frame_shift[0:1], none, frame_shift[1:2]])]
    slice x1 -> x0, local copies, waits for them, and re-layouts: 1.31 us -> none  [on_device(): shifts = jnp.concatenate([none, frame_shift[0:1], none, frame_shift[1:2]])]
    broadcast_in_dim x1 -> x0, local copies, waits for them, and re-layouts: 0.68 us -> none  [on_device(): shifts = jnp.broadcast_to(shifts[:, None, None], (STEPS, ny, nl))]
where the time goes in v2:
time: 36.3 us; the launch traced here: 36.1 us
  Pallas kernels  31.2 us (86%)
  local copies, waits for them, and re-layouts  4.17 us (11%)
  between operations  0.65 us (2%)
    pallas_call x1, Pallas kernels, on_device(): pl.pallas_call(kernel, out_shape=(jax.ShapeDtypeStruct(phase_noise.shape,...  31.2 us
    unnamed x10, local copies, waits for them, and re-layouts  4.17 us

profile of v2, /device:TPU:0, one launch (start us, length us, event | category | flops | bytes accessed | tf_op | source)
XLA Modules:
  0.0 36.1 jit_solution(3861220540047367116)
XLA Ops:
  0.6 0.0 copy-start
  0.6 0.8 %copy-done = f32[4,4,8,128]{3,2,1,0:T(8,128)S(1)} copy-done((f32[4,4,8,128]{3,2,1,0:T(8,128)S(1)}, f32[4,4,8,128]{3,2,1,0:T(8,128)}, u32[]{:S(2)}) %copy-start) | copy-done | bytes 65560
  1.5 0.0 copy-start.1
  1.5 0.8 %copy-done.1 = f32[2,4,8,128]{3,2,1,0:T(8,128)S(1)} copy-done((f32[2,4,8,128]{3,2,1,0:T(8,128)S(1)}, f32[2,4,8,128]{3,2,1,0:T(8,128)}, u32[]{:S(2)}) %copy-start.1) | copy-done | bytes 32792
  2.2 0.0 copy-start.2
  2.2 0.7 %copy-done.2 = s32[4,8]{1,0:T(4,128)S(1)} copy-done((s32[4,8]{1,0:T(4,128)S(1)}, s32[4,8]{1,0:T(4,128)}, u32[]{:S(2)}) %copy-start.2) | copy-done | bytes 152
  2.9 0.0 copy-start.3
  2.9 0.7 %copy-done.3 = s32[2]{0:T(128)S(1)} copy-done((s32[2]{0:T(128)S(1)}, s32[2]{0:T(128)}, u32[]{:S(2)}) %copy-start.3) | copy-done | bytes 32
  3.6 31.2 %eutectic.1 = (f32[4,4,8,128]{3,2,1,0:T(8,128)S(1)}, f32[2,4,8,128]{3,2,1,0:T(8,128)S(1)}) custom-call(s32[4,8]{1,0:T(4,128)S(1)} %copy-done.2, f32[4,4,8,128]{3,2,1,0:T(8,128)S(1)} %copy-done, f32[2,4,8,128]{3,2,1,0:T(8,128)S(1)} %copy-done.1, s32[2]{0:T(128)S(1)} %copy-done.3), custom_call_target="tpu_custom_call" | custom-call | tf_op jit(solution)/shard_map/eutectic/pallas_call | solution.py:377
  34.8 0.6 %copy.8 = f32[4,4,8,128]{3,2,1,0:T(8,128)} copy(f32[4,4,8,128]{3,2,1,0:T(8,128)S(1)} %get-tuple-element.4) | data formatting | bytes 131072
  35.5 0.6 %copy.9 = f32[2,4,8,128]{3,2,1,0:T(8,128)} copy(f32[2,4,8,128]{3,2,1,0:T(8,128)S(1)} %get-tuple-element.5) | data formatting | bytes 65536
Async XLA Ops:
  0.6 0.8 %copy-start = (f32[4,4,8,128]{3,2,1,0:T(8,128)S(1)}, f32[4,4,8,128]{3,2,1,0:T(8,128)}, u32[]{:S(2)}) copy-start(f32[4,4,8,128]{3,2,1,0:T(8,128)} %noise_hbm.1) | copy-start | bytes 196612
  1.5 0.8 %copy-start.1 = (f32[2,4,8,128]{3,2,1,0:T(8,128)S(1)}, f32[2,4,8,128]{3,2,1,0:T(8,128)}, u32[]{:S(2)}) copy-start(f32[2,4,8,128]{3,2,1,0:T(8,128)} %pot_hbm.1) | copy-start | bytes 98308
  2.2 0.7 %copy-start.2 = (s32[4,8]{1,0:T(4,128)S(1)}, s32[4,8]{1,0:T(4,128)}, u32[]{:S(2)}) copy-start(s32[4,8]{1,0:T(4,128)} %labels_hbm.1) | copy-start | bytes 388
  2.9 0.7 %copy-start.3 = (s32[2]{0:T(128)S(1)}, s32[2]{0:T(128)}, u32[]{:S(2)}) copy-start(s32[2]{0:T(128)} %shift_hbm.1) | copy-start | bytes 28

commit v3 on v2

--- a/solution.py
+++ b/solution.py
@@ -210,11 +210,11 @@
             launch(copy(ysnd.at[t, 1], yrcv.at[t, 1], 11, {"gy": ys[1]}))
 
         if not shifted:
-            send_own()
             for x in range(rows):
                 for f in range(5):
                     pack_own(x, f, W[t, f, x + 2, OWN])
             send_y()
+            send_own()
         for c in zcopies:
             c.wait_recv()
         if shifted:
@@ -251,12 +251,13 @@
         xzsnd[t, 0] = packed[0]
         xzsnd[t, 1] = packed[rows - 1]
         if shifted:
-            send_own()
             send_y()
         launch(copy(xzsnd.at[t, 0], xzrcv.at[t, 0], 12, {"gx": xs[-1]}))
         launch(copy(xzsnd.at[t, 1], xzrcv.at[t, 1], 13, {"gx": xs[1]}))
         launch(copy(yzsnd.at[t, 0], yzrcv.at[t, 0], 14, {"gy": ys[-1]}))
         launch(copy(yzsnd.at[t, 1], yzrcv.at[t, 1], 15, {"gy": ys[1]}))
+        if shifted:
+            send_own()
         for c in copies:
             c.wait_recv()
 
@@ -376,10 +377,7 @@
     zrows = -(-3 * rows // ny)
     return pl.pallas_call(
         kernel,
-        out_shape=(
-            jax.ShapeDtypeStruct(phase_noise.shape, f32),
-            jax.ShapeDtypeStruct(potentials.shape, f32),
-        ),
+        out_shape=(pltpu.VMEM(phase_noise.shape, f32), pltpu.VMEM(potentials.shape, f32)),
         in_specs=[hbm] * 4,
         out_specs=(vmem, vmem),
         scratch_shapes=[
@@ -402,9 +400,7 @@
             pltpu.SemaphoreType.DMA((STEPS, 16)),
             pltpu.SemaphoreType.DMA((STEPS, 16)),
         ],
-        compiler_params=pltpu.CompilerParams(
-            collective_id=0, has_side_effects=True, vmem_limit_bytes=16 * 1024 * 1024
-        ),
+        compiler_params=pltpu.CompilerParams(collective_id=0, has_side_effects=True),
         name="eutectic",
     )(labels, phase_noise, potentials, frame_shift)
 

time: 36.3 us -> 33.2 us (0.915)
  local copies, waits for them, and re-layouts: 4.17 us -> 1.25 us
    unnamed x10 -> x2, local copies, waits for them, and re-layouts: 4.17 us -> 1.25 us
where the time goes in v3:
time: 33.2 us; the launch traced here: 33.1 us
  Pallas kernels  31.2 us (94%)
  local copies, waits for them, and re-layouts  1.25 us (4%)
  between operations  0.64 us (2%)
    pallas_call x1, Pallas kernels, on_device(): pl.pallas_call(kernel, out_shape=(pltpu.VMEM(phase_noise.shape, f32), plt...  31.2 us
    unnamed x2, local copies, waits for them, and re-layouts  1.25 us

profile of v3, /device:TPU:0, one launch (start us, length us, event | category | flops | bytes accessed | tf_op | source)
XLA Modules:
  0.0 33.1 jit_solution(1242602875249274120)
XLA Ops:
  0.6 31.2 %eutectic.1 = (f32[4,4,8,128]{3,2,1,0:T(8,128)S(1)}, f32[2,4,8,128]{3,2,1,0:T(8,128)S(1)}) custom-call(s32[4,8]{1,0:T(4,128)} %labels_hbm.1, f32[4,4,8,128]{3,2,1,0:T(8,128)} %noise_hbm.1, f32[2,4,8,128]{3,2,1,0:T(8,128)} %pot_hbm.1, s32[2]{0:T(128)} %shift_hbm.1), custom_call_target="tpu_custom_call" | custom-call | tf_op jit(solution)/shard_map/eutectic/pallas_call | solution.py:378
  31.8 0.6 %copy.8 = f32[4,4,8,128]{3,2,1,0:T(8,128)} copy(f32[4,4,8,128]{3,2,1,0:T(8,128)S(1)} %get-tuple-element.2) | data formatting | bytes 131072
  32.4 0.6 %copy.9 = f32[2,4,8,128]{3,2,1,0:T(8,128)} copy(f32[2,4,8,128]{3,2,1,0:T(8,128)S(1)} %get-tuple-element.3) | data formatting | bytes 65536

commit v4 on v3

--- a/solution.py
+++ b/solution.py
@@ -84,7 +84,7 @@
 
 def kernel(labels_hbm, noise_hbm, pot_hbm, shift_hbm, phase_out, pot_out,
            labels_ref, noise_ref, pot_ref, shift_ref, in_sem,
-           S, W, zrcv, ysnd, yrcv, yzsnd, yzrcv, xzsnd, xzrcv, csnd, crcv, send_sem, recv_sem):
+           S, W, zrcv, ysnd, yrcv, yzsnd, yzrcv, xzsnd, xzrcv, csnd, crcv, czsnd, czrcv, send_sem, recv_sem):
     fetches = [
         pltpu.make_async_copy(src, dst, in_sem.at[n])
         for n, (src, dst) in enumerate(
@@ -200,8 +200,10 @@
                 edge_src = 2 if side < 0 else rows + 1
                 edge_dst = rows + 2 if side < 0 else 1
                 target = {"gx": xs[side]}
-                launch(copy(W.at[t, pl.ds(0, 3), pl.ds(src, 2), OWN], W.at[t, pl.ds(0, 3), pl.ds(dst, 2), OWN], base, target))
-                launch(copy(W.at[t, pl.ds(3, 2), edge_src, OWN], W.at[t, pl.ds(3, 2), edge_dst, OWN], base + 1, target))
+                faces = S.at[t // 2, pl.ds(0, 3), pl.ds(src - 2, 2)] if shifted else W.at[t, pl.ds(0, 3), pl.ds(src, 2), OWN]
+                chem = S.at[t // 2, pl.ds(3, 2), edge_src - 2] if shifted else W.at[t, pl.ds(3, 2), edge_src, OWN]
+                launch(copy(faces, W.at[t, pl.ds(0, 3), pl.ds(dst, 2), OWN], base, target))
+                launch(copy(chem, W.at[t, pl.ds(3, 2), edge_dst, OWN], base + 1, target))
 
         def send_y():
             for n, (i, j) in enumerate(corners):
@@ -209,79 +211,146 @@
             launch(copy(ysnd.at[t, 0], yrcv.at[t, 0], 10, {"gy": ys[-1]}))
             launch(copy(ysnd.at[t, 1], yrcv.at[t, 1], 11, {"gy": ys[1]}))
 
-        if not shifted:
-            for x in range(rows):
-                for f in range(5):
-                    pack_own(x, f, W[t, f, x + 2, OWN])
-            send_y()
-            send_own()
+        def source(x, f):
+            return S[t // 2, f, x] if shifted else W[t, f, x + 2, OWN]
+
+        for x in range(rows):
+            for f in range(5):
+                pack_own(x, f, source(x, f))
+        send_y()
+        send_own()
         for c in zcopies:
             c.wait_recv()
+
+        def clamp(own, halo):
+            first = jnp.broadcast_to(own[:, 0:1], (ny, nl))
+            last = jnp.broadcast_to(own[:, nl - 1 : nl], (ny, nl))
+            halo = jnp.where(upper & (lane < nl // 2), last, halo)
+            return jnp.where(lower & (lane >= nl // 2), first, halo)
+
         if shifted:
             shift = jnp.full((ny, nl), jnp.where(t == 1, first_shift, second_shift), jnp.int32)
             bits = [(shift & 1) != 0, (shift & 2) != 0, (shift & 4) != 0, (shift & 8) != 0]
-        packed = {}
-        for x in range(rows):
-            for f in range(5):
-                own = S[t // 2, f, x] if shifted else W[t, f, x + 2, OWN]
-                halo = jnp.where(lane < nl // 2, zrcv[t, 1, f, x], zrcv[t, 0, f, x])
+
+        def moved(own, halo):
+            for bit in range(4):
+                by = 1 << bit
+                mixed_own = jnp.where(lane < by, halo, own)
+                mixed_halo = jnp.where(lane < by, own, halo)
+                own = jnp.where(bits[bit], pltpu.roll(mixed_own, nl - by, 1), own)
+                halo = jnp.where(bits[bit], pltpu.roll(mixed_halo, nl - by, 1), halo)
+            return own, halo
+
+        def roll_by(value, by):
+            return pltpu.roll(value, by % nl, 1) if by % nl else value
+
+        packed = [None, None]
+
+        def pack_edge(side, at, width, low, value):
+            inside = (lane >= width * at - low) & (lane < width * (at + 1) - low)
+            if at == 0:
+                packed[side] = value
+            else:
+                packed[side] = jnp.where(inside, roll_by(value, width * at), packed[side])
+
+        for f in range(5):
+            for x in range(rows):
                 if shifted:
-                    halo = jnp.where(upper & (lane < nl // 2), 0.0, halo)
-                    for bit in range(4):
-                        by = 1 << bit
-                        mixed_own = jnp.where(lane < by, halo, own)
-                        mixed_halo = jnp.where(lane < by, own, halo)
-                        own = jnp.where(bits[bit], pltpu.roll(mixed_own, nl - by, 1), own)
-                        halo = jnp.where(bits[bit], pltpu.roll(mixed_halo, nl - by, 1), halo)
-                    W[t, f, x + 2, OWN] = own
-                    pack_own(x, f, own)
-                first = jnp.broadcast_to(own[:, 0:1], (ny, nl))
-                last = jnp.broadcast_to(own[:, nl - 1 : nl], (ny, nl))
-                halo = jnp.where(upper & (lane < nl // 2), last, halo)
-                halo = jnp.where(lower & (lane >= nl // 2), first, halo)
-                W[t, f, x + 2, ZH] = halo
-                if f < 3:
-                    at = f * rows + x
-                    yzsnd[t, 0, at // ny, at % ny : at % ny + 1, :] = halo[0:1]
-                    yzsnd[t, 1, at // ny, at % ny : at % ny + 1, :] = halo[ny - 1 : ny]
-                    if x == 0 or x == rows - 1:
-                        mixed = halo if f == 0 else jnp.where(
-                            (lane == 8 * f) | (lane == 8 * f - 1), pltpu.roll(halo, 8 * f, 1), packed[x])
-                        packed[x] = mixed
+                    above = jnp.where(upper, 0.0, zrcv[t, 1, f, x])
+                    if f < 3:
+                        yzsnd[t, 0, f, 2 * x : 2 * x + 2, :] = above[0:2]
+                        yzsnd[t, 1, f, 2 * x : 2 * x + 2, :] = above[ny - 2 : ny]
+                        for n, (i, j) in enumerate(corners):
+                            if x == (0 if i < 0 else rows - 1):
+                                czsnd[t, n, f : f + 1, :] = above[0:1] if j < 0 else above[ny - 1 : ny]
+                        if x < 2:
+                            pack_edge(0, 2 * f + x, 16, 0, above)
+                        if x >= rows - 2 and (f or x == rows - 1):
+                            pack_edge(1, 2 * f + (rows - 1 - x), 16, 0, above)
+                    else:
+                        at = (f - 3) * rows + x
+                        yzsnd[t, 0, 3, at : at + 1, :] = above[0:1]
+                        yzsnd[t, 1, 3, at : at + 1, :] = above[ny - 1 : ny]
+                        if x == 0:
+                            pack_edge(0, 6 + f - 3, 16, 0, above)
+                        if x == rows - 1:
+                            pack_edge(1, 6 + f - 3, 16, 0, above)
+                    if f == 0 and x == rows - 1:
+                        second = jnp.where(upper, 0.0, zrcv[t, 1, 0, rows - 2])
+                        pack_edge(1, 1, 16, 0, second)
+                else:
+                    own = source(x, f)
+                    halo = clamp(own, jnp.where(lane < nl // 2, zrcv[t, 1, f, x], zrcv[t, 0, f, x]))
+                    W[t, f, x + 2, ZH] = halo
+                    if f < 3:
+                        yzsnd[t, 0, f, 2 * x : 2 * x + 1, :] = halo[0:1]
+                        yzsnd[t, 1, f, 2 * x + 1 : 2 * x + 2, :] = halo[ny - 1 : ny]
+                        if x == 0:
+                            pack_edge(0, f, 8, 1, halo)
+                        if x == rows - 1:
+                            pack_edge(1, f, 8, 1, halo)
         xzsnd[t, 0] = packed[0]
-        xzsnd[t, 1] = packed[rows - 1]
+        xzsnd[t, 1] = packed[1]
         if shifted:
-            send_y()
+            for n, (i, j) in enumerate(corners):
+                launch(copy(czsnd.at[t, n], czrcv.at[t, n], 16 + n, {"gx": xs[i], "gy": ys[j]}))
+        launch(copy(yzsnd.at[t, 0], yzrcv.at[t, 0], 14, {"gy": ys[-1]}))
+        launch(copy(yzsnd.at[t, 1], yzrcv.at[t, 1], 15, {"gy": ys[1]}))
         launch(copy(xzsnd.at[t, 0], xzrcv.at[t, 0], 12, {"gx": xs[-1]}))
         launch(copy(xzsnd.at[t, 1], xzrcv.at[t, 1], 13, {"gx": xs[1]}))
-        launch(copy(yzsnd.at[t, 0], yzrcv.at[t, 0], 14, {"gy": ys[-1]}))
-        launch(copy(yzsnd.at[t, 1], yzrcv.at[t, 1], 15, {"gy": ys[1]}))
         if shifted:
-            send_own()
+            for x in range(rows):
+                for f in range(5):
+                    above = jnp.where(upper, 0.0, zrcv[t, 1, f, x])
+                    halo = jnp.where(lane < nl // 2, above, zrcv[t, 0, f, x])
+                    own, halo = moved(source(x, f), halo)
+                    W[t, f, x + 2, OWN] = own
+                    W[t, f, x + 2, ZH] = clamp(own, halo)
         for c in copies:
             c.wait_recv()
 
-        for f in range(3):
-            by = 8 * f
-            for slot, xdst in ((0, rows + 2), (1, 1)):
-                halo = xzrcv[t, slot]
-                W[t, f, xdst, ZH] = pltpu.roll(halo, nl - by, 1) if by else halo
-        for x in range(rows):
-            for f in range(3):
-                W[t, f, x + 2, YH, 0:2, :] = yrcv[t, 0, f, 2 * x : 2 * x + 2, :]
-                W[t, f, x + 2, YH, ny - 2 : ny, :] = yrcv[t, 1, f, 2 * x : 2 * x + 2, :]
-                at = f * rows + x
-                W[t, f, x + 2, YZ, 0:1, :] = yzrcv[t, 0, at // ny, at % ny : at % ny + 1, :]
-                W[t, f, x + 2, YZ, ny - 1 : ny, :] = yzrcv[t, 1, at // ny, at % ny : at % ny + 1, :]
-            for k in range(2):
-                at = k * rows + x
-                W[t, 3 + k, x + 2, YH, 0:1, :] = yrcv[t, 0, 3, at : at + 1, :]
-                W[t, 3 + k, x + 2, YH, ny - 1 : ny, :] = yrcv[t, 1, 3, at : at + 1, :]
+        for slot, edge, outer in ((0, rows + 2, rows + 3), (1, 1, 0)):
+            halo_pack = xzrcv[t, slot]
+            for f in range(5):
+                if not shifted:
+                    if f < 3:
+                        W[t, f, edge, ZH] = roll_by(halo_pack, nl - 8 * f)
+                    continue
+                at = 2 * f if f < 3 else 6 + f - 3
+                own, halo = moved(W[t, f, edge, OWN], roll_by(halo_pack, nl - 16 * at))
+                W[t, f, edge, OWN] = own
+                if f < 3:
+                    W[t, f, edge, ZH] = clamp(own, halo)
+                    W[t, f, outer, OWN] = moved(W[t, f, outer, OWN], roll_by(halo_pack, nl - 16 * (at + 1)))[0]
+
+        for f in range(4):
+            faces = []
+            for slot in range(2):
+                own, halo = yrcv[t, slot, f], yzrcv[t, slot, f]
+                if shifted:
+                    own, halo = moved(own, halo)
+                    if f < 3:
+                        halo = clamp(own, halo)
+                faces.append((own, halo))
+            for x in range(rows):
+                if f < 3:
+                    W[t, f, x + 2, YH, 0:2, :] = faces[0][0][2 * x : 2 * x + 2]
+                    W[t, f, x + 2, YH, ny - 2 : ny, :] = faces[1][0][2 * x : 2 * x + 2]
+                    W[t, f, x + 2, YZ, 0:1, :] = faces[0][1][2 * x : 2 * x + 1]
+                    W[t, f, x + 2, YZ, ny - 1 : ny, :] = faces[1][1][2 * x + 1 : 2 * x + 2]
+                else:
+                    for k in range(2):
+                        at = k * rows + x
+                        W[t, 3 + k, x + 2, YH, 0:1, :] = faces[0][0][at : at + 1]
+                        W[t, 3 + k, x + 2, YH, ny - 1 : ny, :] = faces[1][0][at : at + 1]
         for n, (i, j) in enumerate(corners):
             xdst = rows + 2 if i < 0 else 1
             ydst = 0 if j < 0 else ny - 1
+            own = crcv[t, n]
+            if shifted:
+                own, _ = moved(own, czrcv[t, n])
             for f in range(3):
-                W[t, f, xdst, YH, ydst : ydst + 1, :] = crcv[t, n, f : f + 1, :]
+                W[t, f, xdst, YH, ydst : ydst + 1, :] = own[f : f + 1]
 
         def field(x, q, fs=(0, 1, 2)):
             return [W[t, f, x, q] for f in fs]
@@ -374,7 +443,6 @@
     vmem = pl.BlockSpec(memory_space=pltpu.VMEM)
     hbm = pl.BlockSpec(memory_space=pltpu.HBM)
     f32 = jnp.float32
-    zrows = -(-3 * rows // ny)
     return pl.pallas_call(
         kernel,
         out_shape=(pltpu.VMEM(phase_noise.shape, f32), pltpu.VMEM(potentials.shape, f32)),
@@ -391,14 +459,16 @@
             pltpu.VMEM((STEPS, 2, 5, rows, ny, nl), f32),
             pltpu.VMEM((STEPS, 2, 4, ny, nl), f32),
             pltpu.VMEM((STEPS, 2, 4, ny, nl), f32),
-            pltpu.VMEM((STEPS, 2, zrows, ny, nl), f32),
-            pltpu.VMEM((STEPS, 2, zrows, ny, nl), f32),
+            pltpu.VMEM((STEPS, 2, 4, ny, nl), f32),
+            pltpu.VMEM((STEPS, 2, 4, ny, nl), f32),
             pltpu.VMEM((STEPS, 2, ny, nl), f32),
             pltpu.VMEM((STEPS, 2, ny, nl), f32),
             pltpu.VMEM((STEPS, 4, ny, nl), f32),
             pltpu.VMEM((STEPS, 4, ny, nl), f32),
-            pltpu.SemaphoreType.DMA((STEPS, 16)),
-            pltpu.SemaphoreType.DMA((STEPS, 16)),
+            pltpu.VMEM((STEPS, 4, ny, nl), f32),
+            pltpu.VMEM((STEPS, 4, ny, nl), f32),
+            pltpu.SemaphoreType.DMA((STEPS, 20)),
+            pltpu.SemaphoreType.DMA((STEPS, 20)),
         ],
         compiler_params=pltpu.CompilerParams(collective_id=0, has_side_effects=True),
         name="eutectic",

time: 33.2 us -> 34.1 us (1.027)
  Pallas kernels: 31.2 us -> 32 us
    pallas_call x1, Pallas kernels: 31.2 us -> 32 us  [on_device(): pl.pallas_call(kernel, out_shape=(pltpu.VMEM(phase_noise.shape, f32), plt...]
where the time goes in v4:
time: 34.1 us; the launch traced here: 33.9 us
  Pallas kernels  32 us (94%)
  local copies, waits for them, and re-layouts  1.25 us (4%)
  between operations  0.64 us (2%)
    pallas_call x1, Pallas kernels, on_device(): pl.pallas_call(kernel, out_shape=(pltpu.VMEM(phase_noise.shape, f32), plt...  32 us
    unnamed x2, local copies, waits for them, and re-layouts  1.25 us

profile of v4, /device:TPU:0, one launch (start us, length us, event | category | flops | bytes accessed | tf_op | source)
XLA Modules:
  0.0 33.9 jit_solution(12477764777265191782)
XLA Ops:
  0.6 32.0 %eutectic.1 = (f32[4,4,8,128]{3,2,1,0:T(8,128)S(1)}, f32[2,4,8,128]{3,2,1,0:T(8,128)S(1)}) custom-call(s32[4,8]{1,0:T(4,128)} %labels_hbm.1, f32[4,4,8,128]{3,2,1,0:T(8,128)} %noise_hbm.1, f32[2,4,8,128]{3,2,1,0:T(8,128)} %pot_hbm.1, s32[2]{0:T(128)} %shift_hbm.1), custom_call_target="tpu_custom_call" | custom-call | tf_op jit(solution)/shard_map/eutectic/pallas_call | solution.py:446
  32.7 0.6 %copy.8 = f32[4,4,8,128]{3,2,1,0:T(8,128)} copy(f32[4,4,8,128]{3,2,1,0:T(8,128)S(1)} %get-tuple-element.2) | data formatting | bytes 131072
  33.3 0.6 %copy.9 = f32[2,4,8,128]{3,2,1,0:T(8,128)} copy(f32[2,4,8,128]{3,2,1,0:T(8,128)S(1)} %get-tuple-element.3) | data formatting | bytes 65536

commit v5 on v4

--- a/solution.py
+++ b/solution.py
@@ -229,16 +229,13 @@
             return jnp.where(lower & (lane >= nl // 2), first, halo)
 
         if shifted:
-            shift = jnp.full((ny, nl), jnp.where(t == 1, first_shift, second_shift), jnp.int32)
-            bits = [(shift & 1) != 0, (shift & 2) != 0, (shift & 4) != 0, (shift & 8) != 0]
+            amount = jnp.where(t == 1, first_shift, second_shift)
+            shift = jnp.full((ny, nl), amount, jnp.int32)
 
         def moved(own, halo):
-            for bit in range(4):
-                by = 1 << bit
-                mixed_own = jnp.where(lane < by, halo, own)
-                mixed_halo = jnp.where(lane < by, own, halo)
-                own = jnp.where(bits[bit], pltpu.roll(mixed_own, nl - by, 1), own)
-                halo = jnp.where(bits[bit], pltpu.roll(mixed_halo, nl - by, 1), halo)
+            keep = lane < nl - shift
+            own, halo = pltpu.roll(own, nl - amount, 1), pltpu.roll(halo, nl - amount, 1)
+            own, halo = jnp.where(keep, own, halo), jnp.where(keep, halo, own)
             return own, halo
 
         def roll_by(value, by):

time: 34.1 us -> 33.4 us (0.979)
  Pallas kernels: 32 us -> 31.3 us
    pallas_call x1, Pallas kernels: 32 us -> 31.3 us  [on_device(): pl.pallas_call(kernel, out_shape=(pltpu.VMEM(phase_noise.shape, f32), plt...]
where the time goes in v5:
time: 33.4 us; the launch traced here: 33.2 us
  Pallas kernels  31.3 us (94%)
  local copies, waits for them, and re-layouts  1.25 us (4%)
  between operations  0.64 us (2%)
    pallas_call x1, Pallas kernels, on_device(): pl.pallas_call(kernel, out_shape=(pltpu.VMEM(phase_noise.shape, f32), plt...  31.3 us
    unnamed x2, local copies, waits for them, and re-layouts  1.25 us

profile of v5, /device:TPU:0, one launch (start us, length us, event | category | flops | bytes accessed | tf_op | source)
XLA Modules:
  0.0 33.2 jit_solution(3768676756146229813)
XLA Ops:
  0.6 31.3 %eutectic.1 = (f32[4,4,8,128]{3,2,1,0:T(8,128)S(1)}, f32[2,4,8,128]{3,2,1,0:T(8,128)S(1)}) custom-call(s32[4,8]{1,0:T(4,128)} %labels_hbm.1, f32[4,4,8,128]{3,2,1,0:T(8,128)} %noise_hbm.1, f32[2,4,8,128]{3,2,1,0:T(8,128)} %pot_hbm.1, s32[2]{0:T(128)} %shift_hbm.1), custom_call_target="tpu_custom_call" | custom-call | tf_op jit(solution)/shard_map/eutectic/pallas_call | solution.py:443
  31.9 0.6 %copy.8 = f32[4,4,8,128]{3,2,1,0:T(8,128)} copy(f32[4,4,8,128]{3,2,1,0:T(8,128)S(1)} %get-tuple-element.2) | data formatting | bytes 131072
  32.6 0.6 %copy.9 = f32[2,4,8,128]{3,2,1,0:T(8,128)} copy(f32[2,4,8,128]{3,2,1,0:T(8,128)S(1)} %get-tuple-element.3) | data formatting | bytes 65536
